TPU v7x, 512 devices: a whole 4x4x16 slice. The times are simulated.
512 devices in a mesh: tiles: 32 (over z, core), feat: 16 (over y, x).
Axes of the slice: x: 4, y: 4, z: 16, core: 2. Of those that a mesh axis runs over, the one named last changes fastest.
Arguments:
- feats: bfloat16 [1024, 256, 128], P('tiles', 'feat'), may hold values from -6 to 6
- weight: bfloat16 [128, 128], P('feat'), may hold values from -0.5 to 0.5
- bias: float32 [128], replicated, may hold values from -3 to 3
- neighbours: int32 [1024, 16], P('tiles'), may hold values from 0 to 1023, as said below
- counts: int32 [1024], P('tiles'), may hold values from 4 to 16, as said below
- adj_words: int32 [1024, 16, 24, 256], P('tiles', 'feat'), may hold values from 0 to 2047, as said below
- tile_row: int32 [1024], replicated, may hold values from 0 to 1023, as said below
Outputs:
- new_feats: bfloat16 [1024, 256, 128], P('tiles', 'feat')
Inputs may be any that keep to these rules, and one draw needn't show every extreme that they name: A permutation of the slide's tiles; slide tile s is stored in the same band as its id, tile_row[s] // 32 == s // 32. Slide ids run row by row over a grid of 8 tile columns. If tile_row[s] == r, every neighbours[r, k] lies within 2 grid rows and 2 grid columns of s (grid row = id // 8, column = id % 8). Slots at or past counts[r] hold valid ids that are not used. `counts`: some tile has all 16 slots live in every draw. `adj_words`: word w holds source cells 11 w to 11 w + 10 in its bits 0 to 10; bits for cells 256 and beyond are zero.
All inputs are finite; a program needn't handle non-finite values.
Results may differ from a plain program's by a relative error of at most 0.0031.
Values may be sent and summed in bfloat16 or wider, within the bound.
A program may use at most 64 MiB of HBM per device.

v0:
```python
import jax
import jax.numpy as jnp
from jax import lax
from jax.sharding import PartitionSpec as P

GRID_COLS = 8


def joined_along(parts, dim):
    parts = jnp.moveaxis(parts, 0, dim)
    dims = parts.shape
    return parts.reshape(*dims[:dim], dims[dim] * dims[dim + 1], *dims[dim + 2 :])


def copy_for_each(shard, axis):
    copies = jnp.broadcast_to(shard, (lax.axis_size(axis), *shard.shape))
    return lax.all_to_all(copies, axis, split_axis=0, concat_axis=0, tiled=True)


def gather_directly(shard, axis, dim):
    return joined_along(copy_for_each(shard, axis), dim)


def padded(shard, sides, width):
    for axis, dim in sides:
        devices, length = (lax.axis_size(axis), shard.shape[dim])
        up = [(i, (i + 1) % devices) for i in range(devices - 1)]
        down = [(j, i) for i, j in up]
        last = lax.slice_in_dim(shard, length - width, length, axis=dim)
        initial = lax.slice_in_dim(shard, 0, width, axis=dim)
        before = lax.ppermute(last, axis, up)
        after = lax.ppermute(initial, axis, down)
        shard = jnp.concatenate([before, shard, after], axis=dim)
    return shard


def in_one_piece(arrays, axis, dim, along):
    columns = [a.reshape(*a.shape[:along], -1) for a in arrays]
    both = jnp.concatenate(columns, axis=along)
    result, at, done = (lax.psum_scatter(both, axis, scatter_dimension=dim, tiled=True), 0, [])
    for a, column in zip(arrays, columns):
        share = result[..., at : at + column.shape[along]]
        done.append(share.reshape(*share.shape[:along], *a.shape[along:]))
        at += column.shape[along]
    return tuple(done)


def unpack_bits(packed, cell_count):
    shifts = jnp.arange(11, dtype=jnp.int32)
    bit_values = packed[:, :, None, :] >> shifts[None, None, :, None] & 1
    unrolled = bit_values.reshape(packed.shape[0], packed.shape[1] * 11, packed.shape[2])
    return unrolled[:, :cell_count, :].astype(jnp.bfloat16)


def add_slot(extended, words, local_places, live_slots, slot_index):
    cell_count = extended.shape[1]
    mask_block = unpack_bits(words[:, slot_index], cell_count) * live_slots[:, slot_index][
        :, None, None
    ].astype(jnp.bfloat16)
    gathered = extended[local_places[:, slot_index]]
    running = jnp.einsum("tjd,tjf->tdf", mask_block, gathered, preferred_element_type=jnp.float32)
    degree = jnp.sum(mask_block, axis=1, dtype=jnp.float32)
    return (running, degree)


def per_device(feats, weight, bias, neighbours, counts, adj_words, tile_row):
    tiles_here = feats.shape[0]
    features = feats.shape[2]
    whole, weight_full = (gather_directly(feats, "feat", 1), gather_directly(weight, "feat", 0))
    tile_rank = lax.axis_index("tiles")
    first_row = tile_rank * tiles_here
    margin = 2 * GRID_COLS
    own_rows = lax.dynamic_slice_in_dim(tile_row, first_row, tiles_here) - first_row
    ordered = whole[own_rows]
    extended = padded(ordered, (("tiles", 0),), margin)
    places = neighbours - (first_row - margin)
    slots_here = adj_words.shape[1]
    slot_base = lax.axis_index("feat") * slots_here
    local_places = lax.dynamic_slice_in_dim(places, slot_base, slots_here, 1)
    slot_ids = slot_base + jnp.arange(slots_here, dtype=jnp.int32)
    live_slots = slot_ids[None, :] < counts[:, None]
    dest_cells = adj_words.shape[3]
    state_pair = (
        jnp.zeros((tiles_here, dest_cells, features), jnp.float32),
        jnp.zeros((tiles_here, dest_cells), jnp.float32),
    )
    state_pair = add_slot(extended, adj_words, local_places, live_slots, 0)
    summed_rows, degree_rows = in_one_piece((state_pair[0], state_pair[1]), "feat", 1, 2)
    base = feats.astype(jnp.float32)
    normed = ((summed_rows + base) / jnp.sqrt(degree_rows + 1.0)[:, :, None]).astype(jnp.bfloat16)
    linear = (
        jnp.dot(normed.reshape(-1, features), weight_full, preferred_element_type=jnp.float32)
        + bias
    )
    result = base.reshape(-1, features) + jax.nn.relu(linear)
    return result.astype(jnp.bfloat16).reshape(feats.shape)


def solution(mesh):
    return jax.shard_map(
        per_device,
        mesh=mesh,
        in_specs=(
            P("tiles", "feat", None),
            P("feat", None),
            P(),
            P("tiles", None),
            P("tiles"),
            P("tiles", "feat", None, None),
            P(),
        ),
        out_specs=P("tiles", "feat", None),
        check_vma=False,
    )
```

profile of v0, /device:TPU:1, one launch (start us, length us, event | category | flops | bytes accessed | tf_op | source)
XLA Modules:
  0.0 208.2 jit_solution(7574626672843374132)
XLA Ops:
  6.5 2.6 %broadcast_in_dim.6 = bf16[16,32,16,128]{3,2,1,0:T(8,128)(2,1)} broadcast(bf16[32,16,128]{2,1,0:T(8,128)(2,1)} %param.7), dimensions={1,2,3} | broadcast | bytes 2228224 | tf_op jit(solution)/shard_map/broadcast_in_dim | solution.py:16
  9.2 7.6 %all-to-all-start = ((bf16[16,32,16,128]{3,2,1,0:T(8,128)(2,1)}), bf16[16,32,16,128]{3,2,1,0:T(8,128)(2,1)S(1)}, u32[]{:S(2)}, u32[]{:S(2)}) async-start(bf16[16,32,16,128]{3,2,1,0:T(8,128)(2,1)} %broadcast_in_dim.6), calls=%async_computation | async-start | bytes 4194304 | tf_op jit(solution)/shard_map/all_to_all | solution.py:17
  16.8 0.0 reduce-scatter.2.cloned.1.call-start
  16.8 0.1 shift_right_arithmetic.26
  16.9 0.0 copy-start.1
  16.9 1.4 copy.22
  18.3 0.8 compare_select_fusion.1
  19.1 22.9 %all-to-all-done = bf16[16,32,16,128]{3,2,1,0:T(8,128)(2,1)S(1)} async-done(((bf16[16,32,16,128]{3,2,1,0:T(8,128)(2,1)}), bf16[16,32,16,128]{3,2,1,0:T(8,128)(2,1)S(1)}, u32[]{:S(2)}, u32[]{:S(2)}) %all-to-all-start) | async-done | bytes 2097184 | tf_op jit(solution)/shard_map/all_to_all | solution.py:17
  42.0 1.9 copy.23
  44.0 0.0 copy-start.4
  44.0 2.6 %gather_fusion = bf16[32,256,128]{2,1,0:T(8,128)(2,1)S(1)} fusion(bf16[32,256,128]{2,1,0:T(8,128)(2,1)} %bitcast.19, s32[1024]{0:T(1024)S(1)} %pad_clamp_fusion.1), kind=kCustom, calls=%fused_computation | custom fusion | bytes 4194432 | tf_op jit(solution)/shard_map/gather | solution.py:74
  46.5 0.0 copy-done.1
  46.5 1.5 fusion.13
  48.0 7.7 %collective-permute-start.1 = (bf16[16,256,128]{2,1,0:T(8,128)(2,1)}, bf16[16,256,128]{2,1,0:T(8,128)(2,1)}, u32[]{:S(2)}, u32[]{:S(2)}) collective-permute-start(bf16[16,256,128]{2,1,0:T(8,128)(2,1)} %get-tuple-element.8), channel_id=1, source_target_pairs={{16,0},{32,16},{48,32},{64,48},{80,64},{96,80},{112,96},{128,112},... | collective-permute-start | bytes 3145736 | tf_op jit(solution)/shard_map/ppermute | solution.py:32
  55.7 5.1 %collective-permute-start = (bf16[16,256,128]{2,1,0:T(8,128)(2,1)}, bf16[16,256,128]{2,1,0:T(8,128)(2,1)}, u32[]{:S(2)}, u32[]{:S(2)}) collective-permute-start(bf16[16,256,128]{2,1,0:T(8,128)(2,1)} %get-tuple-element.7), channel_id=1, source_target_pairs={{0,16},{16,32},{32,48},{48,64},{64,80},{80,96},{96,112},{112,128},... | collective-permute-start | bytes 3145736 | tf_op jit(solution)/shard_map/ppermute | solution.py:31
  60.8 0.0 copy-done.4
  60.8 0.0 slice-start
  60.8 1.1 shift_right_arithmetic.23
  62.0 0.0 slice-done
  62.0 3.2 %convert_reduce_fusion = (f32[32,256]{1,0:T(8,128)S(1)}, bf16[32,256,256]{2,0,1:T(8,128)(2,1)}) fusion(bf16[32]{0:T(256)(128)(2,1)S(1)} %compare_convert_fusion, s32[256]{0:T(256)S(1)} %slice-done, s32[32,264,256]{2,0,1:T(8,128)S(1)} %bitcast.18), kind=kLoop, calls=%fused_computation.5 | loop fusion | flops 18866176 | bytes 12616768 | tf_op jit(solution)/shard_map/reduce_sum | solution.py:62
  65.2 0.7 fusion.11
  65.9 5.8 %collective-permute-done.1 = bf16[16,256,128]{2,1,0:T(8,128)(2,1)} collective-permute-done((bf16[16,256,128]{2,1,0:T(8,128)(2,1)}, bf16[16,256,128]{2,1,0:T(8,128)(2,1)}, u32[]{:S(2)}, u32[]{:S(2)}) %collective-permute-start.1) | collective-permute-done | bytes 1048608 | tf_op jit(solution)/shard_map/ppermute | solution.py:32
  71.7 1.2 collective-permute-done
  72.8 3.5 %pad_maximum_fusion.1 = bf16[64,256,128]{2,1,0:T(8,128)(2,1)} fusion(bf16[16,256,128]{2,1,0:T(8,128)(2,1)} %collective-permute-done.1, bf16[32,256,128]{2,1,0:T(8,128)(2,1)S(1)} %gather_fusion, bf16[16,256,128]{2,1,0:T(8,128)(2,1)} %collective-permute-done), kind=kLoop, calls=%fused_computation.8 | loop fusion | flops 4194304 | bytes 8388608 | tf_op jit(solution)/shard_map/concatenate | solution.py:33
  76.4 3.1 %gather_fusion.1 = bf16[32,256,128]{2,1,0:T(8,128)(2,1)S(1)} fusion(bf16[64,256,128]{2,1,0:T(8,128)(2,1)} %pad_maximum_fusion.1, s32[1024]{0:T(1024)S(1)} %pad_clamp_fusion), kind=kCustom, calls=%fused_computation.1 | custom fusion | bytes 4194432 | tf_op jit(solution)/shard_map/gather | solution.py:60
  79.5 4.9 %fusion.3 = f32[32,256,128]{1,2,0:T(8,128)S(1)} fusion(bf16[32,256,128]{2,1,0:T(8,128)(2,1)S(1)} %gather_fusion.1, bf16[32,256,256]{2,0,1:T(8,128)(2,1)} %get-tuple-element.6), kind=kOutput, calls=%fused_computation.9 | convolution fusion | flops 536870912 | bytes 10485760 | tf_op jit(solution)/shard_map/tjd,tjf->tdf/dot_general | solution.py:61
  84.4 2.4 %pad_maximum_fusion = f32[32,256,129]{1,2,0:T(8,128)} fusion(f32[32,256,1]{1,2,0:T(1,128)S(1)} %reshape.36, f32[32,256,128]{1,2,0:T(8,128)S(1)} %fusion.3), kind=kLoop, calls=%fused_computation.6 | loop fusion | flops 1056768 | bytes 8454144 | tf_op jit(solution)/shard_map/concatenate | solution.py:39
  86.8 8.7 %copy.26 = f32[32,256,129]{2,0,1:T(8,128)} copy(f32[32,256,129]{1,2,0:T(8,128)} %pad_maximum_fusion) | data formatting | bytes 8454144 | tf_op jit(solution)/shard_map/concatenate | solution.py:39
  95.6 0.0 copy-start.2
  95.6 0.0 copy-start
  95.6 0.0 copy-start.3
  95.6 0.0 reduce-scatter.2.cloned.1.call-update
  95.6 0.7 copy-done.2
  96.2 0.6 broadcast_in_dim.16
  96.9 3.5 %all-to-all-start.1 = ((bf16[16,8,128]{2,1,0:T(8,128)(2,1)}), bf16[16,8,128]{2,1,0:T(8,128)(2,1)S(1)}, u32[]{:S(2)}, u32[]{:S(2)}) async-start(bf16[16,8,128]{2,1,0:T(8,128)(2,1)} %broadcast_in_dim.16), calls=%async_computation.2 | async-start | bytes 65536 | tf_op jit(solution)/shard_map/all_to_all | solution.py:17
  100.4 97.7 %reduce-scatter.2.cloned.1.call-done = f32[32,16,129]{2,0,1:T(8,128)} async-done(((f32[32,256,129]{2,0,1:T(8,128)}), f32[32,16,129]{2,0,1:T(8,128)}) %reduce-scatter.2.cloned.1.call-update) | async-done | bytes 264208 | tf_op jit(solution)/shard_map/reduce_scatter | solution.py:40
  198.1 1.0 slice.30
  199.1 0.2 copy.32
  199.2 0.1 copy.29
  199.3 1.0 slice.29
  200.3 0.0 copy-done
  200.3 0.2 fusion.9
  200.5 0.0 all-to-all-done.1
  200.5 0.0 copy-done.3
  200.5 0.8 fusion.7
  (6 shorter events, 0.1 us)
Async XLA Ops:
  9.2 32.9 %all-to-all-start = ((bf16[16,32,16,128]{3,2,1,0:T(8,128)(2,1)}), bf16[16,32,16,128]{3,2,1,0:T(8,128)(2,1)S(1)}, u32[]{:S(2)}, u32[]{:S(2)}) async-start(bf16[16,32,16,128]{3,2,1,0:T(8,128)(2,1)} %broadcast_in_dim.6), calls=%async_computation | async-start | bytes 4194304 | tf_op jit(solution)/shard_map/all_to_all | solution.py:17
  16.8 181.3 %reduce-scatter.2.cloned.1.call-start = ((), (), s32[]{:S(2)}) async-start(), calls=%async_computation.3 | async-start | bytes 8912896 | tf_op jit(solution)/shard_map/reduce_scatter | solution.py:40
  16.9 29.6 %copy-start.1 = (s32[264]{0:T(512)}, s32[264]{0:T(512)S(1)}, u32[]{:S(2)}) copy-start(s32[264]{0:T(512)S(1)} %shift_right_arithmetic.26) | copy-start | bytes 3172
  44.0 16.8 %copy-start.4 = (s32[32]{0:T(128)S(1)}, s32[32]{0:T(128)}, u32[]{:S(2)}) copy-start(s32[32]{0:T(128)} %param.11) | copy-start | bytes 388
  48.0 23.6 %collective-permute-start.1 = (bf16[16,256,128]{2,1,0:T(8,128)(2,1)}, bf16[16,256,128]{2,1,0:T(8,128)(2,1)}, u32[]{:S(2)}, u32[]{:S(2)}) collective-permute-start(bf16[16,256,128]{2,1,0:T(8,128)(2,1)} %get-tuple-element.8), channel_id=1, source_target_pairs={{16,0},{32,16},{48,32},{64,48},{80,64},{96,80},{112,96},{128,112},... | collective-permute-start | bytes 3145736 | tf_op jit(solution)/shard_map/ppermute | solution.py:32
  55.7 17.1 %collective-permute-start = (bf16[16,256,128]{2,1,0:T(8,128)(2,1)}, bf16[16,256,128]{2,1,0:T(8,128)(2,1)}, u32[]{:S(2)}, u32[]{:S(2)}) collective-permute-start(bf16[16,256,128]{2,1,0:T(8,128)(2,1)} %get-tuple-element.7), channel_id=1, source_target_pairs={{0,16},{16,32},{32,48},{48,64},{64,80},{80,96},{96,112},{112,128},... | collective-permute-start | bytes 3145736 | tf_op jit(solution)/shard_map/ppermute | solution.py:31
  60.8 1.1 slice-start
  95.6 0.7 copy-start.2
  95.6 104.7 %copy-start = (bf16[32,16,128]{2,1,0:T(8,128)(2,1)S(1)}, bf16[32,16,128]{2,1,0:T(8,128)(2,1)}, u32[]{:S(2)}) copy-start(bf16[32,16,128]{2,1,0:T(8,128)(2,1)} %param.7) | copy-start | bytes 393220
  95.6 105.0 %copy-start.3 = (f32[128]{0:T(128)S(1)}, f32[128]{0:T(128)}, u32[]{:S(2)}) copy-start(f32[128]{0:T(128)} %param.9) | copy-start | bytes 1540
  96.9 103.6 %all-to-all-start.1 = ((bf16[16,8,128]{2,1,0:T(8,128)(2,1)}), bf16[16,8,128]{2,1,0:T(8,128)(2,1)S(1)}, u32[]{:S(2)}, u32[]{:S(2)}) async-start(bf16[16,8,128]{2,1,0:T(8,128)(2,1)} %broadcast_in_dim.16), calls=%async_computation.2 | async-start | bytes 65536 | tf_op jit(solution)/shard_map/all_to_all | solution.py:17
Sparse Core Ops, SparseCore 0:
  95.7 102.3 reduce-scatter.1
where the time goes:
time: 209 us; the launch traced here: 208 us
  waiting for transfers between devices  128 us (61%)
  local copies, waits for them, and re-layouts  26.5 us (13%)
  starting transfers between devices  23.9 us (11%)
  between operations  13.6 us (7%)
  other arithmetic  10.8 us (5%)
  matrix products  5.76 us (3%)
    reduce_scatter x1, waiting for transfers between devices, in_one_piece(): lax.psum_scatter(both, axis, scatter_dimension=dim, tiled=True)  97.7 us
    all_to_all x2, waiting for transfers between devices, copy_for_each(): return lax.all_to_all(copies, axis, split_axis=0, concat_axis=0, tiled=True)  23 us
    all_to_all x2, starting transfers between devices, copy_for_each(): return lax.all_to_all(copies, axis, split_axis=0, concat_axis=0, tiled=True)  11.1 us
    concatenate x1, local copies, waits for them, and re-layouts, in_one_piece(): both = jnp.concatenate(columns, axis=along)  8.73 us
    ppermute x1, starting transfers between devices, padded(): after = lax.ppermute(initial, axis, down)  7.68 us
    ppermute x1, waiting for transfers between devices, padded(): after = lax.ppermute(initial, axis, down)  5.78 us
    ppermute x1, starting transfers between devices, padded(): before = lax.ppermute(last, axis, up)  5.1 us
    dot_general x1, matrix products, add_slot(): jnp.einsum('tjd,tjf->tdf', mask_block, gathered, preferred_element_type=j...  4.92 us
  transfers between devices with their start and end apart: 5, of which 4 were waited for; matrix products, arithmetic and copies ran while one was open for 5% of the time, Pallas kernels for 0%

commit v1 on v0

v1 whole, which is shorter than its diff:
```python
import functools

import jax
import jax.numpy as jnp
from jax import lax
from jax.experimental import pallas as pl
from jax.experimental.pallas import tpu as pltpu
from jax.sharding import PartitionSpec as P

MESH = pl.DeviceIdType.MESH
BF16 = jnp.bfloat16
F32 = jnp.float32
I32 = jnp.int32

SLOTS = 16
CELLS = 256
CHUNK = 16
WORDS = 24
BITS = 11
LANES = 128
TILES = 32
WIN_ROWS = 5
WIN_COLS = 6


def kernel(
    n_tiles,
    feats_hbm, weight_hbm, bias_ref, nb_hbm, words_hbm, counts_ref, rows_ref,
    out_ref,
    feats_v, words_v, weight_v, nb_own, nb_other, stage_f, stage_w, win, wbuf, wall, bits32, mask, feats_t, stage_o, obuf, inverse,
    local_sem, nb_send, nb_sem, word_send, word_sem, weight_send, weight_sem, win_send, win_sem, fwd_send, fwd_sem, out_send, out_sem,
):
    t = lax.axis_index("tiles")
    f = lax.axis_index("feat")
    z = t // 2
    core = t % 2
    partner = 2 * z + 1 - core
    row_in_plane = f // 2
    half = f % 2
    home = f // 8
    dest_row = 8 * z + row_in_plane
    n_planes = n_tiles // 2

    def device(tiles, feat):
        return {"tiles": tiles, "feat": feat}

    loads = [
        pltpu.make_async_copy(words_hbm, words_v, local_sem.at[0]),
        pltpu.make_async_copy(feats_hbm, feats_v, local_sem.at[1]),
        pltpu.make_async_copy(weight_hbm, weight_v, local_sem.at[2]),
        pltpu.make_async_copy(nb_hbm, nb_own, local_sem.at[3]),
    ]
    for load in loads:
        load.start()

    barrier = pltpu.get_barrier_semaphore()

    def greet(i, carry):
        tiles, feat = 2 * z + i // 16, i % 16

        @pl.when(jnp.logical_or(tiles != t, feat != f))
        def _():
            pl.semaphore_signal(barrier, inc=1, device_id=device(tiles, feat), device_id_type=MESH)

        return carry

    lax.fori_loop(0, 32, greet, 0)

    needs_before = jnp.logical_and(row_in_plane < 2, z > 0)
    needs_after = jnp.logical_and(row_in_plane >= 6, z < n_planes - 1)

    def greet_halo(tiles):
        def body(i, carry):
            pl.semaphore_signal(barrier, inc=1, device_id=device(tiles, core * 8 + i), device_id_type=MESH)
            return carry

        lax.fori_loop(0, 8, body, 0)

    @pl.when(needs_before)
    def _():
        greet_halo(2 * z - 1)

    @pl.when(needs_after)
    def _():
        greet_halo(2 * z + 2)

    for load in loads:
        load.wait()

    def order(s, carry):
        row = jnp.clip(rows_ref[t * TILES + s] - t * TILES, 0, TILES - 1)
        live = f < counts_ref[row]
        w = words_v[row]
        packed = w[:, :LANES] | (w[:, LANES:] << 16)
        stage_w[s] = jnp.where(live, packed, jnp.zeros_like(packed))
        stage_f[s // 8, s % 8] = feats_v[row]
        return carry

    lax.fori_loop(0, TILES, order, 0)

    sends_beyond = jnp.logical_or(
        jnp.logical_and(core == 1, z < n_planes - 1), jnp.logical_and(core == 0, z > 0)
    )

    @pl.when(sends_beyond)
    def _():
        pl.semaphore_wait(barrier, 35)

    @pl.when(jnp.logical_not(sends_beyond))
    def _():
        pl.semaphore_wait(barrier, 31)

    nb_copy = pltpu.make_async_remote_copy(
        nb_own, nb_other, nb_send, nb_sem, device_id=device(partner, f), device_id_type=MESH
    )
    nb_copy.start()

    def word_copy(i):
        chip = core * 8 + (i // 2 + f) % 8
        side = i % 2
        first = 4 * (chip % 8) + 2 * side
        mine = jnp.logical_and(chip == f, side == core)
        copy = pltpu.make_async_remote_copy(
            stage_w.at[pl.ds(first, 2)], wbuf.at[f], word_send.at[i], word_sem.at[f],
            device_id=device(2 * z + side, chip), device_id_type=MESH,
        )
        return copy, mine, first

    def start_words(i, carry):
        copy, mine, first = word_copy(i)

        @pl.when(jnp.logical_not(mine))
        def _():
            copy.start()

        @pl.when(mine)
        def _():
            wbuf[f] = stage_w[pl.ds(first, 2)]

        return carry

    lax.fori_loop(0, 16, start_words, 0)

    weight_mine = weight_v[...]
    wall[f] = weight_mine

    def weight_copy(i):
        chip = (f + i) % 16
        return pltpu.make_async_remote_copy(
            weight_v, wall.at[f], weight_send.at[i], weight_sem.at[f],
            device_id=device(t, chip), device_id_type=MESH,
        )

    def start_weight(i, carry):
        weight_copy(i).start()
        return carry

    lax.fori_loop(1, 16, start_weight, 0)

    my_cells = pl.ds(pl.multiple_of(f * CHUNK, CHUNK), CHUNK)

    def feat_copy(i):
        combo = (i // 4 + row_in_plane) % 10
        step = combo // 2 - 2
        h = combo % 2
        r = i % 4
        to_row = 4 * t + r + step
        valid = jnp.logical_and(to_row >= 0, to_row < 4 * n_tiles)
        tiles = 2 * (to_row // 8) + f // 8
        chip = 2 * (to_row % 8) + h
        mine = jnp.logical_and(tiles == t, chip == f)
        copy = pltpu.make_async_remote_copy(
            stage_f.at[r, pl.ds(2 * h, WIN_COLS)],
            win.at[2 - step, :, my_cells],
            win_send.at[i], win_sem.at[2 - step, f % 8],
            device_id=device(tiles, chip), device_id_type=MESH,
        )
        return copy, valid, mine, r, h, step

    def start_feats(i, carry):
        copy, valid, mine, r, h, step = feat_copy(i)

        @pl.when(jnp.logical_and(valid, jnp.logical_not(mine)))
        def _():
            copy.start()

        @pl.when(jnp.logical_and(valid, mine))
        def _():
            win[2 - step, :, my_cells] = stage_f[r, pl.ds(2 * h, WIN_COLS)]

        return carry

    lax.fori_loop(0, 40, start_feats, 0)

    def invert(r, carry):
        def look(s, found):
            return found + jnp.where(rows_ref[t * TILES + s] == t * TILES + r, s, 0)

        inverse[r] = jnp.clip(lax.fori_loop(0, TILES, look, 0), 0, TILES - 1)
        return carry

    lax.fori_loop(0, TILES, invert, 0)

    def row_exists(w):
        row = dest_row + w - 2
        return jnp.logical_and(row >= 0, row < 4 * n_tiles)

    def clear(w, carry):
        @pl.when(jnp.logical_not(row_exists(w)))
        def _():
            win[w] = jnp.zeros((WIN_COLS, CELLS, LANES), BF16)

        return carry

    lax.fori_loop(0, WIN_ROWS, clear, 0)

    ones_rows = jnp.ones((16, CELLS), BF16)

    def fill_ones(i, carry):
        feats_t[i, pl.ds(LANES, 16)] = ones_rows
        return carry

    lax.fori_loop(0, WIN_ROWS * WIN_COLS, fill_ones, 0)

    def unpack(k, carry):
        @pl.when(jnp.logical_not(jnp.logical_and(k == f, core == home)))
        def _():
            pltpu.make_async_copy(wbuf.at[k], wbuf.at[k], word_sem.at[k]).wait()

        for tile in range(2):
            packed = wbuf[k, tile]
            for b in range(BITS):
                bits32[0, pl.ds(b, WORDS, stride=BITS), :] = (packed >> b) & 1
                bits32[1, pl.ds(b, WORDS, stride=BITS), :] = (packed >> (16 + b)) & 1
            mask[tile, k, :, :LANES] = bits32[0, :CELLS].astype(F32).astype(BF16)
            mask[tile, k, :, LANES:] = bits32[1, :CELLS].astype(F32).astype(BF16)
        return carry

    lax.fori_loop(0, SLOTS, unpack, 0)

    kept = pl.ds(pl.multiple_of(core * LANES, LANES), LANES)

    def forward_copy(w):
        return pltpu.make_async_remote_copy(
            win.at[w, :, kept], win.at[w, :, kept], fwd_send.at[w], fwd_sem.at[w],
            device_id=device(partner, f), device_id_type=MESH,
        )

    def forward(w, carry):
        @pl.when(row_exists(w))
        def _():
            local = jnp.logical_and(home == core, (dest_row + w - 2) // 4 == t)

            def arrive(i, c):
                @pl.when(jnp.logical_not(jnp.logical_and(local, i == f % 8)))
                def _():
                    cells = pl.ds(pl.multiple_of((core * 8 + i) * CHUNK, CHUNK), CHUNK)
                    pltpu.make_async_copy(
                        win.at[w, :, cells], win.at[w, :, cells], win_sem.at[w, i]
                    ).wait()

                return c

            lax.fori_loop(0, 8, arrive, 0)
            forward_copy(w).start()

        return carry

    lax.fori_loop(0, WIN_ROWS, forward, 0)

    def turn(w, carry):
        @pl.when(row_exists(w))
        def _():
            forward_copy(w).wait_recv()

        for c in range(WIN_COLS):
            feats_t[w * WIN_COLS + c, pl.ds(0, LANES)] = win[w, c].T
        return carry

    lax.fori_loop(0, WIN_ROWS, turn, 0)

    nb_copy.wait_recv()

    def weight_wait(i, carry):
        chip = (f + i) % 16
        pltpu.make_async_copy(wall.at[chip], wall.at[chip], weight_sem.at[chip]).wait()
        return carry

    lax.fori_loop(1, 16, weight_wait, 0)
    weight = wall[...].astype(F32).reshape(LANES, LANES).astype(BF16)
    bias = bias_ref[...]
    band = 2 * z + home

    for tile in range(2):
        slide = 4 * (f % 8) + 2 * core + tile
        row = jnp.clip(rows_ref[band * TILES + slide] - band * TILES, 0, TILES - 1)

        def add(k, acc):
            near = jnp.where(home == core, nb_own[row, k], nb_other[row, k])
            place = (near // 8 - (dest_row - 2)) * WIN_COLS + near % 8 - 2 * half
            place = jnp.clip(place, 0, WIN_ROWS * WIN_COLS - 1)
            return acc + jnp.dot(feats_t[place], mask[tile, k], preferred_element_type=F32)

        total = lax.fori_loop(0, SLOTS, add, jnp.zeros((LANES + 16, CELLS), F32)).T
        base = win[2, 4 * half + 2 * core + tile - 2 * half].astype(F32)
        degree = total[:, LANES : LANES + 1]
        normed = ((total[:, :LANES] + base) / jnp.sqrt(degree + 1.0)).astype(BF16)
        linear = jnp.dot(normed, weight, preferred_element_type=F32) + bias
        stage_o[tile] = (base + jnp.maximum(linear, 0.0)).astype(BF16)

    first_out = 4 * (f % 8) + 2 * core

    def out_copy(i):
        chip = (f + i) % 16
        cells = pl.ds(pl.multiple_of(chip * CHUNK, CHUNK), CHUNK)
        mine = jnp.logical_and(i == 0, home == core)
        copy = pltpu.make_async_remote_copy(
            stage_o.at[:, cells], obuf.at[pl.ds(first_out, 2)], out_send.at[i], out_sem.at[first_out // 2],
            device_id=device(2 * z + home, chip), device_id_type=MESH,
        )
        return copy, mine

    def start_out(i, carry):
        copy, mine = out_copy(i)

        @pl.when(jnp.logical_not(mine))
        def _():
            copy.start()

        @pl.when(mine)
        def _():
            obuf[pl.ds(first_out, 2)] = stage_o[:, my_cells]

        return carry

    lax.fori_loop(0, 16, start_out, 0)

    nb_copy.wait_send()

    def end_words(i, carry):
        copy, mine, _ = word_copy(i)

        @pl.when(jnp.logical_not(mine))
        def _():
            copy.wait_send()

        return carry

    lax.fori_loop(0, 16, end_words, 0)

    def end_weight(i, carry):
        weight_copy(i).wait_send()
        return carry

    lax.fori_loop(1, 16, end_weight, 0)

    def end_feats(i, carry):
        copy, valid, mine, _, _, _ = feat_copy(i)

        @pl.when(jnp.logical_and(valid, jnp.logical_not(mine)))
        def _():
            copy.wait_send()

        return carry

    lax.fori_loop(0, 40, end_feats, 0)

    def end_forward(w, carry):
        @pl.when(row_exists(w))
        def _():
            forward_copy(w).wait_send()

        return carry

    lax.fori_loop(0, WIN_ROWS, end_forward, 0)

    def end_out(i, carry):
        copy, mine = out_copy(i)

        @pl.when(jnp.logical_not(mine))
        def _():
            copy.wait_send()

        return carry

    lax.fori_loop(0, 16, end_out, 0)

    def arrive_out(i, carry):
        @pl.when(jnp.logical_not(jnp.logical_and(home == core, i == first_out // 2)))
        def _():
            pair = pl.ds(2 * i, 2)
            pltpu.make_async_copy(obuf.at[pair], obuf.at[pair], out_sem.at[i]).wait()

        return carry

    lax.fori_loop(0, 16, arrive_out, 0)

    def put(r, carry):
        out_ref[r] = obuf[inverse[r]]
        return carry

    lax.fori_loop(0, TILES, put, 0)


def solution(mesh):
    n_tiles = mesh.shape["tiles"]

    def per_device(feats, weight, bias, neighbours, counts, adj_words, tile_row):
        vmem = pl.BlockSpec(memory_space=pltpu.VMEM)
        smem = pl.BlockSpec(memory_space=pltpu.SMEM)
        hbm = pl.BlockSpec(memory_space=pl.ANY)
        words = adj_words.reshape(TILES, WORDS, CELLS)
        return pl.pallas_call(
            functools.partial(kernel, n_tiles),
            out_shape=jax.ShapeDtypeStruct(feats.shape, BF16),
            in_specs=[hbm, hbm, vmem, hbm, hbm, smem, smem],
            out_specs=vmem,
            scratch_shapes=[
                pltpu.VMEM((TILES, CHUNK, LANES), BF16),
                pltpu.VMEM((TILES, WORDS, CELLS), I32),
                pltpu.VMEM((8, LANES), BF16),
                pltpu.SMEM((TILES, SLOTS), I32),
                pltpu.SMEM((TILES, SLOTS), I32),
                pltpu.VMEM((4, 8, CHUNK, LANES), BF16),
                pltpu.VMEM((TILES, WORDS, LANES), I32),
                pltpu.VMEM((WIN_ROWS, WIN_COLS, CELLS, LANES), BF16),
                pltpu.VMEM((SLOTS, 2, WORDS, LANES), I32),
                pltpu.VMEM((16, 8, LANES), BF16),
                pltpu.VMEM((2, WORDS * BITS, LANES), I32),
                pltpu.VMEM((2, SLOTS, CELLS, CELLS), BF16),
                pltpu.VMEM((WIN_ROWS * WIN_COLS, LANES + 16, CELLS), BF16),
                pltpu.VMEM((2, CELLS, LANES), BF16),
                pltpu.VMEM((TILES, CHUNK, LANES), BF16),
                pltpu.SMEM((TILES,), I32),
                pltpu.SemaphoreType.DMA((4,)),
                pltpu.SemaphoreType.DMA,
                pltpu.SemaphoreType.DMA,
                pltpu.SemaphoreType.DMA((16,)),
                pltpu.SemaphoreType.DMA((SLOTS,)),
                pltpu.SemaphoreType.DMA((16,)),
                pltpu.SemaphoreType.DMA((16,)),
                pltpu.SemaphoreType.DMA((40,)),
                pltpu.SemaphoreType.DMA((WIN_ROWS, 8)),
                pltpu.SemaphoreType.DMA((WIN_ROWS,)),
                pltpu.SemaphoreType.DMA((WIN_ROWS,)),
                pltpu.SemaphoreType.DMA((16,)),
                pltpu.SemaphoreType.DMA((16,)),
            ],
            compiler_params=pltpu.CompilerParams(collective_id=0, has_side_effects=True),
        )(feats, weight, bias.reshape(1, LANES), neighbours, words, counts, tile_row)

    return jax.shard_map(
        per_device,
        mesh=mesh,
        in_specs=(
            P("tiles", "feat", None),
            P("feat", None),
            P(),
            P("tiles", None),
            P("tiles"),
            P("tiles", "feat", None, None),
            P(),
        ),
        out_specs=P("tiles", "feat", None),
        check_vma=False,
    )
```

time: 209 us -> 48.5 us (0.23)
  waiting for transfers between devices: 128 us -> 0 us
  Pallas kernels: 0 us -> 45.3 us
  starting transfers between devices: 23.9 us -> 0 us
  local copies, waits for them, and re-layouts: 26.5 us -> 2.94 us
  between operations: 13.6 us -> 0.01 us
  other arithmetic: 10.8 us -> 0 us
  matrix products: 5.76 us -> 0 us
    reduce_scatter x1 -> x0, waiting for transfers between devices: 97.7 us -> none  [in_one_piece(): lax.psum_scatter(both, axis, scatter_dimension=dim, tiled=True)]
    pallas_call x0 -> x1, Pallas kernels: none -> 45.3 us  [per_device(): pl.pallas_call(functools.partial(kernel, n_tiles), out_shape=jax.ShapeDty...]
    all_to_all x2 -> x0, waiting for transfers between devices: 23 us -> none  [copy_for_each(): return lax.all_to_all(copies, axis, split_axis=0, concat_axis=0, tiled=True)]
    ppermute x2 -> x0, starting transfers between devices: 12.8 us -> none  [the longest x1 7.68 us: padded(): after = lax.ppermute(initial, axis, down)]
    all_to_all x2 -> x0, starting transfers between devices: 11.1 us -> none  [copy_for_each(): return lax.all_to_all(copies, axis, split_axis=0, concat_axis=0, tiled=True)]
    concatenate x1 -> x0, local copies, waits for them, and re-layouts: 8.73 us -> none  [in_one_piece(): both = jnp.concatenate(columns, axis=along)]
    ppermute x2 -> x0, waiting for transfers between devices: 6.96 us -> none  [the longest x1 5.78 us: padded(): after = lax.ppermute(initial, axis, down)]
    concatenate x2 -> x0, other arithmetic: 5.91 us -> none  [the longest x1 3.52 us: padded(): shard = jnp.concatenate([before, shard, after], axis=dim)]
  transfers between devices with their start and end apart: 5 -> 0, of which waited for: 4 -> 0; matrix products, arithmetic and copies ran while one was open for 5% -> 0% of each run, Pallas kernels for 0% -> 0%
where the time goes in v1:
time: 48.5 us; the launch traced here: 48.3 us
  Pallas kernels  45.3 us (93%)
  local copies, waits for them, and re-layouts  2.94 us (6%)
    pallas_call x1, Pallas kernels, per_device(): pl.pallas_call(functools.partial(kernel, n_tiles), out_shape=jax.ShapeDty...  45.3 us
    unnamed x2, local copies, waits for them, and re-layouts  2.94 us

profile of v1, /device:TPU:1, one launch (start us, length us, event | category | flops | bytes accessed | tf_op | source)
XLA Modules:
  0.0 48.3 jit_solution(12012217564042842330)
XLA Ops:
  0.0 1.4 %copy.8.nb_hbm = s32[32,16]{1,0:T(8,128)} copy(s32[32,16]{0,1:T(8,128)} %param.10) | data formatting | bytes 4096 | tf_op args[3]
  1.4 45.3 %shard_map.73 = bf16[32,16,128]{2,1,0:T(8,128)(2,1)} custom-call(bf16[32,16,128]{2,1,0:T(8,128)(2,1)} %feats_hbm.1, bf16[8,128]{1,0:T(8,128)(2,1)} %weight_hbm.1, f32[1,128]{1,0:T(1,128)} %bitcast.3, s32[32,16]{1,0:T(8,128)} %copy.8.nb_hbm, s32[32,24,256]{2,1,0:T(8,128)} %bitcast.2, s32[32]{0:T(128)} %counts_ref.1, s32[1024]{0:T(1024)} %rows_ref.1), custom_call_target="tpu_custom_call" | custom-call | tf_op jit(solution)/shard_map/pallas_call | solution.py:413
  46.7 1.6 %copy.10 = bf16[32,16,128]{2,1,0:T(8,128)(2,1)} copy(bf16[32,16,128]{2,1,0:T(8,128)(2,1)} %shard_map.73) | data formatting | bytes 262144

commit v2 on v1

--- a/solution.py
+++ b/solution.py
@@ -159,44 +159,35 @@
 
     my_cells = pl.ds(pl.multiple_of(f * CHUNK, CHUNK), CHUNK)
 
-    def feat_copy(i):
-        combo = (i // 4 + row_in_plane) % 10
-        step = combo // 2 - 2
-        h = combo % 2
-        r = i % 4
+    feat_sends = []
+    for i in range(40):
+        step, h, r = i // 8 - 2, i // 4 % 2, i % 4
         to_row = 4 * t + r + step
         valid = jnp.logical_and(to_row >= 0, to_row < 4 * n_tiles)
-        tiles = 2 * (to_row // 8) + f // 8
+        tiles = 2 * (to_row // 8) + home
         chip = 2 * (to_row % 8) + h
-        mine = jnp.logical_and(tiles == t, chip == f)
+        sent = jnp.logical_and(valid, jnp.logical_or(tiles != t, chip != f))
         copy = pltpu.make_async_remote_copy(
             stage_f.at[r, pl.ds(2 * h, WIN_COLS)],
             win.at[2 - step, :, my_cells],
             win_send.at[i], win_sem.at[2 - step, f % 8],
             device_id=device(tiles, chip), device_id_type=MESH,
         )
-        return copy, valid, mine, r, h, step
-
-    def start_feats(i, carry):
-        copy, valid, mine, r, h, step = feat_copy(i)
-
-        @pl.when(jnp.logical_and(valid, jnp.logical_not(mine)))
-        def _():
-            copy.start()
-
-        @pl.when(jnp.logical_and(valid, mine))
-        def _():
-            win[2 - step, :, my_cells] = stage_f[r, pl.ds(2 * h, WIN_COLS)]
-
-        return carry
-
-    lax.fori_loop(0, 40, start_feats, 0)
+        feat_sends.append((copy, sent))
+        pl.when(sent)(copy.start)
+
+    for r in range(4):
+        w = 4 * t + r - dest_row + 2
+
+        @pl.when(jnp.logical_and(home == core, jnp.logical_and(w >= 0, w < WIN_ROWS)))
+        def _():
+            win[w, :, my_cells] = stage_f[r, pl.ds(2 * half, WIN_COLS)]
 
     def invert(r, carry):
-        def look(s, found):
-            return found + jnp.where(rows_ref[t * TILES + s] == t * TILES + r, s, 0)
-
-        inverse[r] = jnp.clip(lax.fori_loop(0, TILES, look, 0), 0, TILES - 1)
+        found = 0
+        for s in range(1, TILES):
+            found = found + jnp.where(rows_ref[t * TILES + s] == t * TILES + r, s, 0)
+        inverse[r] = jnp.clip(found, 0, TILES - 1)
         return carry
 
     lax.fori_loop(0, TILES, invert, 0)
@@ -291,17 +282,24 @@
     bias = bias_ref[...]
     band = 2 * z + home
 
-    for tile in range(2):
-        slide = 4 * (f % 8) + 2 * core + tile
-        row = jnp.clip(rows_ref[band * TILES + slide] - band * TILES, 0, TILES - 1)
-
-        def add(k, acc):
-            near = jnp.where(home == core, nb_own[row, k], nb_other[row, k])
+    firsts = 4 * (f % 8) + 2 * core
+    rows = [
+        jnp.clip(rows_ref[band * TILES + firsts + tile] - band * TILES, 0, TILES - 1) for tile in range(2)
+    ]
+
+    def add(k, totals):
+        done = []
+        for tile in range(2):
+            near = jnp.where(home == core, nb_own[k, rows[tile]], nb_other[k, rows[tile]])
             place = (near // 8 - (dest_row - 2)) * WIN_COLS + near % 8 - 2 * half
             place = jnp.clip(place, 0, WIN_ROWS * WIN_COLS - 1)
-            return acc + jnp.dot(feats_t[place], mask[tile, k], preferred_element_type=F32)
-
-        total = lax.fori_loop(0, SLOTS, add, jnp.zeros((LANES + 16, CELLS), F32)).T
+            done.append(totals[tile] + jnp.dot(feats_t[place], mask[tile, k], preferred_element_type=F32))
+        return tuple(done)
+
+    zero = jnp.zeros((LANES + 16, CELLS), F32)
+    totals = lax.fori_loop(0, SLOTS, add, (zero, zero), unroll=True)
+    for tile in range(2):
+        total = totals[tile].T
         base = win[2, 4 * half + 2 * core + tile - 2 * half].astype(F32)
         degree = total[:, LANES : LANES + 1]
         normed = ((total[:, :LANES] + base) / jnp.sqrt(degree + 1.0)).astype(BF16)
@@ -354,16 +352,8 @@
 
     lax.fori_loop(1, 16, end_weight, 0)
 
-    def end_feats(i, carry):
-        copy, valid, mine, _, _, _ = feat_copy(i)
-
-        @pl.when(jnp.logical_and(valid, jnp.logical_not(mine)))
-        def _():
-            copy.wait_send()
-
-        return carry
-
-    lax.fori_loop(0, 40, end_feats, 0)
+    for copy, sent in feat_sends:
+        pl.when(sent)(copy.wait_send)
 
     def end_forward(w, carry):
         @pl.when(row_exists(w))
@@ -419,8 +409,8 @@
                 pltpu.VMEM((TILES, CHUNK, LANES), BF16),
                 pltpu.VMEM((TILES, WORDS, CELLS), I32),
                 pltpu.VMEM((8, LANES), BF16),
-                pltpu.SMEM((TILES, SLOTS), I32),
-                pltpu.SMEM((TILES, SLOTS), I32),
+                pltpu.SMEM((SLOTS, TILES), I32),
+                pltpu.SMEM((SLOTS, TILES), I32),
                 pltpu.VMEM((4, 8, CHUNK, LANES), BF16),
                 pltpu.VMEM((TILES, WORDS, LANES), I32),
                 pltpu.VMEM((WIN_ROWS, WIN_COLS, CELLS, LANES), BF16),
@@ -447,7 +437,7 @@
                 pltpu.SemaphoreType.DMA((16,)),
             ],
             compiler_params=pltpu.CompilerParams(collective_id=0, has_side_effects=True),
-        )(feats, weight, bias.reshape(1, LANES), neighbours, words, counts, tile_row)
+        )(feats, weight, bias.reshape(1, LANES), neighbours.T, words, counts, tile_row)
 
     return jax.shard_map(
         per_device,

time: 48.5 us -> 41.9 us (0.86)
  Pallas kernels: 45.3 us -> 40.1 us
  local copies, waits for them, and re-layouts: 2.94 us -> 1.57 us
    pallas_call x1, Pallas kernels: 45.3 us -> 40.1 us  [per_device(): pl.pallas_call(functools.partial(kernel, n_tiles), out_shape=jax.ShapeDty...]
    unnamed x2 -> x1, local copies, waits for them, and re-layouts: 2.94 us -> 1.57 us
where the time goes in v2:
time: 41.9 us; the launch traced here: 41.7 us
  Pallas kernels  40.1 us (96%)
  local copies, waits for them, and re-layouts  1.57 us (4%)
    pallas_call x1, Pallas kernels, per_device(): pl.pallas_call(functools.partial(kernel, n_tiles), out_shape=jax.ShapeDty...  40.1 us
    unnamed x1, local copies, waits for them, and re-layouts  1.57 us

profile of v2, /device:TPU:1, one launch (start us, length us, event | category | flops | bytes accessed | tf_op | source)
XLA Modules:
  0.0 41.7 jit_solution(7585993998226520072)
XLA Ops:
  0.0 40.1 %shard_map.73 = bf16[32,16,128]{2,1,0:T(8,128)(2,1)} custom-call(bf16[32,16,128]{2,1,0:T(8,128)(2,1)} %feats_hbm.1, bf16[8,128]{1,0:T(8,128)(2,1)} %weight_hbm.1, f32[1,128]{1,0:T(1,128)} %bitcast.5, s32[16,32]{1,0:T(8,128)} %bitcast.4, s32[32,24,256]{2,1,0:T(8,128)} %bitcast.3, s32[32]{0:T(128)} %counts_ref.1, s32[1024]{0:T(1024)} %rows_ref.1), custom_call_target="tpu_custom_call" | custom-call | tf_op jit(solution)/shard_map/pallas_call | solution.py:403
  40.1 1.6 %copy.9 = bf16[32,16,128]{2,1,0:T(8,128)(2,1)} copy(bf16[32,16,128]{2,1,0:T(8,128)(2,1)} %shard_map.73) | data formatting | bytes 262144

commit v3 on v2

--- a/solution.py
+++ b/solution.py
@@ -8,6 +8,10 @@
 from jax.sharding import PartitionSpec as P
 
 MESH = pl.DeviceIdType.MESH
+STEPS = (
+    (2, 2), (1, 2), (3, 2), (2, 1), (2, 3), (0, 2), (2, 0), (1, 1),
+    (3, 3), (1, 3), (3, 1), (0, 1), (0, 3), (1, 0), (3, 0), (0, 0),
+)
 BF16 = jnp.bfloat16
 F32 = jnp.float32
 I32 = jnp.int32
@@ -25,9 +29,9 @@
 
 def kernel(
     n_tiles,
-    feats_hbm, weight_hbm, bias_ref, nb_hbm, words_hbm, counts_ref, rows_ref,
+    feats_hbm, weight_hbm, bias_hbm, nb_hbm, words_hbm, counts_hbm, rows_hbm,
     out_ref,
-    feats_v, words_v, weight_v, nb_own, nb_other, stage_f, stage_w, win, wbuf, wall, bits32, mask, feats_t, stage_o, obuf, inverse,
+    feats_v, words_v, weight_v, bias_ref, counts_ref, rows_ref, nb_own, nb_other, stage_f, stage_w, win, wbuf, wall, bits32, mask, feats_t, stage_o, obuf, inverse,
     local_sem, nb_send, nb_sem, word_send, word_sem, weight_send, weight_sem, win_send, win_sem, fwd_send, fwd_sem, out_send, out_sem,
 ):
     t = lax.axis_index("tiles")
@@ -49,22 +53,20 @@
         pltpu.make_async_copy(feats_hbm, feats_v, local_sem.at[1]),
         pltpu.make_async_copy(weight_hbm, weight_v, local_sem.at[2]),
         pltpu.make_async_copy(nb_hbm, nb_own, local_sem.at[3]),
+        pltpu.make_async_copy(bias_hbm, bias_ref, local_sem.at[4]),
+        pltpu.make_async_copy(counts_hbm, counts_ref, local_sem.at[5]),
+        pltpu.make_async_copy(rows_hbm, rows_ref, local_sem.at[6]),
     ]
     for load in loads:
         load.start()
 
     barrier = pltpu.get_barrier_semaphore()
 
-    def greet(i, carry):
-        tiles, feat = 2 * z + i // 16, i % 16
-
-        @pl.when(jnp.logical_or(tiles != t, feat != f))
-        def _():
-            pl.semaphore_signal(barrier, inc=1, device_id=device(tiles, feat), device_id_type=MESH)
-
-        return carry
-
-    lax.fori_loop(0, 32, greet, 0)
+    chips = [(f // 4 + dy) % 4 * 4 + (f % 4 + dx) % 4 for dy, dx in STEPS]
+
+    for i, chip in enumerate(chips):
+        for tiles in (partner,) if STEPS[i] == (0, 0) else (t, partner):
+            pl.semaphore_signal(barrier, inc=1, device_id=device(tiles, chip), device_id_type=MESH)
 
     needs_before = jnp.logical_and(row_in_plane < 2, z > 0)
     needs_after = jnp.logical_and(row_in_plane >= 6, z < n_planes - 1)
@@ -115,31 +117,23 @@
     )
     nb_copy.start()
 
-    def word_copy(i):
-        chip = core * 8 + (i // 2 + f) % 8
-        side = i % 2
-        first = 4 * (chip % 8) + 2 * side
-        mine = jnp.logical_and(chip == f, side == core)
-        copy = pltpu.make_async_remote_copy(
-            stage_w.at[pl.ds(first, 2)], wbuf.at[f], word_send.at[i], word_sem.at[f],
-            device_id=device(2 * z + side, chip), device_id_type=MESH,
-        )
-        return copy, mine, first
-
-    def start_words(i, carry):
-        copy, mine, first = word_copy(i)
-
-        @pl.when(jnp.logical_not(mine))
-        def _():
-            copy.start()
-
-        @pl.when(mine)
-        def _():
-            wbuf[f] = stage_w[pl.ds(first, 2)]
-
-        return carry
-
-    lax.fori_loop(0, 16, start_words, 0)
+    word_sends = []
+    for i, chip in enumerate(chips):
+        for side in range(2):
+            sent = chip // 8 == core
+            if STEPS[i] == (0, 0):
+                sent = jnp.logical_and(sent, side != core)
+            copy = pltpu.make_async_remote_copy(
+                stage_w.at[pl.ds(4 * (chip % 8) + 2 * side, 2)], wbuf.at[f],
+                word_send.at[2 * i + side], word_sem.at[f],
+                device_id=device(2 * z + side, chip), device_id_type=MESH,
+            )
+            word_sends.append((copy, sent))
+            pl.when(sent)(copy.start)
+
+    @pl.when(home == core)
+    def _():
+        wbuf[f] = stage_w[pl.ds(4 * (f % 8) + 2 * core, 2)]
 
     weight_mine = weight_v[...]
     wall[f] = weight_mine
@@ -160,21 +154,24 @@
     my_cells = pl.ds(pl.multiple_of(f * CHUNK, CHUNK), CHUNK)
 
     feat_sends = []
-    for i in range(40):
-        step, h, r = i // 8 - 2, i // 4 % 2, i % 4
-        to_row = 4 * t + r + step
-        valid = jnp.logical_and(to_row >= 0, to_row < 4 * n_tiles)
+    for i, chip in enumerate(chips):
+        ahead = jnp.where(core == 0, (chip // 2 + 2) % 8 - 2, (chip // 2 + 6) % 8 - 2)
+        to_row = 4 * t + ahead
+        inside = jnp.logical_and(to_row >= 0, to_row < 4 * n_tiles)
         tiles = 2 * (to_row // 8) + home
-        chip = 2 * (to_row % 8) + h
-        sent = jnp.logical_and(valid, jnp.logical_or(tiles != t, chip != f))
-        copy = pltpu.make_async_remote_copy(
-            stage_f.at[r, pl.ds(2 * h, WIN_COLS)],
-            win.at[2 - step, :, my_cells],
-            win_send.at[i], win_sem.at[2 - step, f % 8],
-            device_id=device(tiles, chip), device_id_type=MESH,
-        )
-        feat_sends.append((copy, sent))
-        pl.when(sent)(copy.start)
+        for r in range(4):
+            sent = jnp.logical_and(inside, jnp.logical_and(ahead - r >= -2, ahead - r <= 2))
+            if STEPS[i] == (0, 0):
+                sent = jnp.logical_and(sent, tiles != t)
+            w = jnp.clip(r - ahead + 2, 0, WIN_ROWS - 1)
+            copy = pltpu.make_async_remote_copy(
+                stage_f.at[r, pl.ds(2 * (chip % 2), WIN_COLS)],
+                win.at[w, :, my_cells],
+                win_send.at[4 * i + r], win_sem.at[w, f % 8],
+                device_id=device(tiles, chip), device_id_type=MESH,
+            )
+            feat_sends.append((copy, sent))
+            pl.when(sent)(copy.start)
 
     for r in range(4):
         w = 4 * t + r - dest_row + 2
@@ -205,10 +202,11 @@
 
     lax.fori_loop(0, WIN_ROWS, clear, 0)
 
-    ones_rows = jnp.ones((16, CELLS), BF16)
+    ones_rows = jnp.ones((16, LANES), BF16)
 
     def fill_ones(i, carry):
-        feats_t[i, pl.ds(LANES, 16)] = ones_rows
+        feats_t[0, i, pl.ds(LANES, 16)] = ones_rows
+        feats_t[1, i, pl.ds(LANES, 16)] = ones_rows
         return carry
 
     lax.fori_loop(0, WIN_ROWS * WIN_COLS, fill_ones, 0)
@@ -229,6 +227,14 @@
 
     lax.fori_loop(0, SLOTS, unpack, 0)
 
+    nb_copy.wait_recv()
+
+    def weight_wait(i, carry):
+        chip = (f + i) % 16
+        pltpu.make_async_copy(wall.at[chip], wall.at[chip], weight_sem.at[chip]).wait()
+        return carry
+
+    lax.fori_loop(1, 16, weight_wait, 0)
     kept = pl.ds(pl.multiple_of(core * LANES, LANES), LANES)
 
     def forward_copy(w):
@@ -259,25 +265,26 @@
 
     lax.fori_loop(0, WIN_ROWS, forward, 0)
 
-    def turn(w, carry):
+    given = pl.ds(pl.multiple_of((1 - core) * LANES, LANES), LANES)
+
+    def turn_kept(w, carry):
+        for c in range(WIN_COLS):
+            feats_t[core, w * WIN_COLS + c, pl.ds(0, LANES)] = win[w, c, kept].T
+        return carry
+
+    lax.fori_loop(0, WIN_ROWS, turn_kept, 0)
+
+    def turn_given(w, carry):
         @pl.when(row_exists(w))
         def _():
             forward_copy(w).wait_recv()
 
         for c in range(WIN_COLS):
-            feats_t[w * WIN_COLS + c, pl.ds(0, LANES)] = win[w, c].T
-        return carry
-
-    lax.fori_loop(0, WIN_ROWS, turn, 0)
-
-    nb_copy.wait_recv()
-
-    def weight_wait(i, carry):
-        chip = (f + i) % 16
-        pltpu.make_async_copy(wall.at[chip], wall.at[chip], weight_sem.at[chip]).wait()
-        return carry
-
-    lax.fori_loop(1, 16, weight_wait, 0)
+            feats_t[1 - core, w * WIN_COLS + c, pl.ds(0, LANES)] = win[w, c, given].T
+        return carry
+
+    lax.fori_loop(0, WIN_ROWS, turn_given, 0)
+
     weight = wall[...].astype(F32).reshape(LANES, LANES).astype(BF16)
     bias = bias_ref[...]
     band = 2 * z + home
@@ -293,7 +300,10 @@
             near = jnp.where(home == core, nb_own[k, rows[tile]], nb_other[k, rows[tile]])
             place = (near // 8 - (dest_row - 2)) * WIN_COLS + near % 8 - 2 * half
             place = jnp.clip(place, 0, WIN_ROWS * WIN_COLS - 1)
-            done.append(totals[tile] + jnp.dot(feats_t[place], mask[tile, k], preferred_element_type=F32))
+            done.append(totals[tile] + jnp.dot(
+                jnp.concatenate([feats_t[0, place], feats_t[1, place]], axis=1), mask[tile, k],
+                preferred_element_type=F32,
+            ))
         return tuple(done)
 
     zero = jnp.zeros((LANES + 16, CELLS), F32)
@@ -308,43 +318,29 @@
 
     first_out = 4 * (f % 8) + 2 * core
 
-    def out_copy(i):
-        chip = (f + i) % 16
+    out_sends = []
+    for i, chip in enumerate(chips):
         cells = pl.ds(pl.multiple_of(chip * CHUNK, CHUNK), CHUNK)
-        mine = jnp.logical_and(i == 0, home == core)
         copy = pltpu.make_async_remote_copy(
-            stage_o.at[:, cells], obuf.at[pl.ds(first_out, 2)], out_send.at[i], out_sem.at[first_out // 2],
+            stage_o.at[:, cells], obuf.at[pl.ds(first_out, 2)],
+            out_send.at[i], out_sem.at[first_out // 2],
             device_id=device(2 * z + home, chip), device_id_type=MESH,
         )
-        return copy, mine
-
-    def start_out(i, carry):
-        copy, mine = out_copy(i)
-
-        @pl.when(jnp.logical_not(mine))
-        def _():
+        sent = home != core if STEPS[i] == (0, 0) else True
+        out_sends.append((copy, sent))
+        if sent is True:
             copy.start()
-
-        @pl.when(mine)
-        def _():
-            obuf[pl.ds(first_out, 2)] = stage_o[:, my_cells]
-
-        return carry
-
-    lax.fori_loop(0, 16, start_out, 0)
+        else:
+            pl.when(sent)(copy.start)
+
+    @pl.when(home == core)
+    def _():
+        obuf[pl.ds(first_out, 2)] = stage_o[:, my_cells]
 
     nb_copy.wait_send()
 
-    def end_words(i, carry):
-        copy, mine, _ = word_copy(i)
-
-        @pl.when(jnp.logical_not(mine))
-        def _():
-            copy.wait_send()
-
-        return carry
-
-    lax.fori_loop(0, 16, end_words, 0)
+    for copy, sent in word_sends:
+        pl.when(sent)(copy.wait_send)
 
     def end_weight(i, carry):
         weight_copy(i).wait_send()
@@ -364,16 +360,11 @@
 
     lax.fori_loop(0, WIN_ROWS, end_forward, 0)
 
-    def end_out(i, carry):
-        copy, mine = out_copy(i)
-
-        @pl.when(jnp.logical_not(mine))
-        def _():
+    for copy, sent in out_sends:
+        if sent is True:
             copy.wait_send()
-
-        return carry
-
-    lax.fori_loop(0, 16, end_out, 0)
+        else:
+            pl.when(sent)(copy.wait_send)
 
     def arrive_out(i, carry):
         @pl.when(jnp.logical_not(jnp.logical_and(home == core, i == first_out // 2)))
@@ -397,18 +388,20 @@
 
     def per_device(feats, weight, bias, neighbours, counts, adj_words, tile_row):
         vmem = pl.BlockSpec(memory_space=pltpu.VMEM)
-        smem = pl.BlockSpec(memory_space=pltpu.SMEM)
         hbm = pl.BlockSpec(memory_space=pl.ANY)
         words = adj_words.reshape(TILES, WORDS, CELLS)
         return pl.pallas_call(
             functools.partial(kernel, n_tiles),
-            out_shape=jax.ShapeDtypeStruct(feats.shape, BF16),
-            in_specs=[hbm, hbm, vmem, hbm, hbm, smem, smem],
+            out_shape=pltpu.VMEM(feats.shape, BF16),
+            in_specs=[hbm] * 7,
             out_specs=vmem,
             scratch_shapes=[
                 pltpu.VMEM((TILES, CHUNK, LANES), BF16),
                 pltpu.VMEM((TILES, WORDS, CELLS), I32),
                 pltpu.VMEM((8, LANES), BF16),
+                pltpu.VMEM((1, LANES), F32),
+                pltpu.SMEM((TILES,), I32),
+                pltpu.SMEM((n_tiles * TILES,), I32),
                 pltpu.SMEM((SLOTS, TILES), I32),
                 pltpu.SMEM((SLOTS, TILES), I32),
                 pltpu.VMEM((4, 8, CHUNK, LANES), BF16),
@@ -418,18 +411,18 @@
                 pltpu.VMEM((16, 8, LANES), BF16),
                 pltpu.VMEM((2, WORDS * BITS, LANES), I32),
                 pltpu.VMEM((2, SLOTS, CELLS, CELLS), BF16),
-                pltpu.VMEM((WIN_ROWS * WIN_COLS, LANES + 16, CELLS), BF16),
+                pltpu.VMEM((2, WIN_ROWS * WIN_COLS, LANES + 16, LANES), BF16),
                 pltpu.VMEM((2, CELLS, LANES), BF16),
                 pltpu.VMEM((TILES, CHUNK, LANES), BF16),
                 pltpu.SMEM((TILES,), I32),
-                pltpu.SemaphoreType.DMA((4,)),
+                pltpu.SemaphoreType.DMA((7,)),
                 pltpu.SemaphoreType.DMA,
                 pltpu.SemaphoreType.DMA,
-                pltpu.SemaphoreType.DMA((16,)),
+                pltpu.SemaphoreType.DMA((32,)),
                 pltpu.SemaphoreType.DMA((SLOTS,)),
                 pltpu.SemaphoreType.DMA((16,)),
                 pltpu.SemaphoreType.DMA((16,)),
-                pltpu.SemaphoreType.DMA((40,)),
+                pltpu.SemaphoreType.DMA((64,)),
                 pltpu.SemaphoreType.DMA((WIN_ROWS, 8)),
                 pltpu.SemaphoreType.DMA((WIN_ROWS,)),
                 pltpu.SemaphoreType.DMA((WIN_ROWS,)),

time: 41.9 us -> 39 us (0.931)
  Pallas kernels: 40.1 us -> 38.2 us
  local copies, waits for them, and re-layouts: 1.57 us -> 0.66 us
    pallas_call x1, Pallas kernels: 40.1 us -> 38.2 us  [per_device(): pl.pallas_call(functools.partial(kernel, n_tiles), out_shape=pltpu.VMEM(f...]
    unnamed x1, local copies, waits for them, and re-layouts: 1.57 us -> 0.66 us
where the time goes in v3:
time: 39 us; the launch traced here: 38.9 us
  Pallas kernels  38.2 us (98%)
  local copies, waits for them, and re-layouts  0.66 us (2%)
    pallas_call x1, Pallas kernels, per_device(): pl.pallas_call(functools.partial(kernel, n_tiles), out_shape=pltpu.VMEM(f...  38.2 us

profile of v3, /device:TPU:1, one launch (start us, length us, event | category | flops | bytes accessed | tf_op | source)
XLA Modules:
  0.0 38.9 jit_solution(16527142838974037014)
XLA Ops:
  0.0 38.2 %shard_map.73 = bf16[32,16,128]{2,1,0:T(8,128)(2,1)S(1)} custom-call(bf16[32,16,128]{2,1,0:T(8,128)(2,1)} %feats_hbm.1, bf16[8,128]{1,0:T(8,128)(2,1)} %weight_hbm.1, f32[1,128]{1,0:T(1,128)} %bitcast.5, s32[16,32]{1,0:T(8,128)} %bitcast.4, s32[32,24,256]{2,1,0:T(8,128)} %bitcast.3, s32[32]{0:T(128)} %counts_hbm.1, s32[1024]{0:T(1024)} %rows_hbm.1), custom_call_target="tpu_custom_call" | custom-call | tf_op jit(solution)/shard_map/pallas_call | solution.py:393
  38.3 0.7 %copy.9 = bf16[32,16,128]{2,1,0:T(8,128)(2,1)} copy(bf16[32,16,128]{2,1,0:T(8,128)(2,1)S(1)} %shard_map.73) | data formatting | bytes 262144

commit v4 on v3

--- a/solution.py
+++ b/solution.py
@@ -31,8 +31,8 @@
     n_tiles,
     feats_hbm, weight_hbm, bias_hbm, nb_hbm, words_hbm, counts_hbm, rows_hbm,
     out_ref,
-    feats_v, words_v, weight_v, bias_ref, counts_ref, rows_ref, nb_own, nb_other, stage_f, stage_w, win, wbuf, wall, bits32, mask, feats_t, stage_o, obuf, inverse,
-    local_sem, nb_send, nb_sem, word_send, word_sem, weight_send, weight_sem, win_send, win_sem, fwd_send, fwd_sem, out_send, out_sem,
+    feats_v, words_v, weight_v, bias_ref, counts_ref, rows_ref, nb_own, nb_other, stage_f, stage_w, relay_y, relay_x, win, wbuf, wall, bits32, mask, feats_t, stage_o, obuf, inverse,
+    local_sem, nb_send, nb_sem, word_send, word_sem, weight_send, weight_sem, to_y_send, to_y_sem, to_x_send, to_x_sem, win_y_send, win_y_sem, win_x_send, win_x_sem, fwd_send, fwd_sem, out_send, out_sem,
 ):
     t = lax.axis_index("tiles")
     f = lax.axis_index("feat")
@@ -40,6 +40,7 @@
     core = t % 2
     partner = 2 * z + 1 - core
     row_in_plane = f // 2
+    y, x = f // 4, f % 4
     half = f % 2
     home = f // 8
     dest_row = 8 * z + row_in_plane
@@ -68,23 +69,36 @@
         for tiles in (partner,) if STEPS[i] == (0, 0) else (t, partner):
             pl.semaphore_signal(barrier, inc=1, device_id=device(tiles, chip), device_id_type=MESH)
 
-    needs_before = jnp.logical_and(row_in_plane < 2, z > 0)
-    needs_after = jnp.logical_and(row_in_plane >= 6, z < n_planes - 1)
-
-    def greet_halo(tiles):
-        def body(i, carry):
-            pl.semaphore_signal(barrier, inc=1, device_id=device(tiles, core * 8 + i), device_id_type=MESH)
-            return carry
-
-        lax.fori_loop(0, 8, body, 0)
-
-    @pl.when(needs_before)
-    def _():
-        greet_halo(2 * z - 1)
-
-    @pl.when(needs_after)
-    def _():
-        greet_halo(2 * z + 2)
+    def plane_for(chip_y):
+        below = jnp.logical_and(core == 0, chip_y == 3).astype(I32)
+        above = jnp.logical_and(core == 1, chip_y == 0).astype(I32)
+        return z - below + above
+
+    def ahead_of(chip_y):
+        return (2 * chip_y + jnp.where(core == 0, 2, 6)) % 8 - 2
+
+    def in_slide(plane):
+        return jnp.logical_and(plane >= 0, plane < n_planes)
+
+    for source_y in range(4):
+        above = jnp.logical_and(y == 3, z < n_planes - 1)
+        below = jnp.logical_and(y == 0, z > 0)
+        if source_y < 2:
+            above = jnp.logical_and(above, core == 0)
+        else:
+            below = jnp.logical_and(below, core == 1)
+
+        @pl.when(above)
+        def _():
+            pl.semaphore_signal(
+                barrier, inc=1, device_id=device(2 * z + 2, 4 * source_y + x), device_id_type=MESH
+            )
+
+        @pl.when(below)
+        def _():
+            pl.semaphore_signal(
+                barrier, inc=1, device_id=device(2 * z - 1, 4 * source_y + x), device_id_type=MESH
+            )
 
     for load in loads:
         load.wait()
@@ -100,17 +114,57 @@
 
     lax.fori_loop(0, TILES, order, 0)
 
-    sends_beyond = jnp.logical_or(
-        jnp.logical_and(core == 1, z < n_planes - 1), jnp.logical_and(core == 0, z > 0)
+    beyond = jnp.where(
+        core == 0, jnp.where(z > 0, 1 + y // 2, 0), jnp.where(z < n_planes - 1, 2 - y // 2, 0)
     )
-
-    @pl.when(sends_beyond)
-    def _():
-        pl.semaphore_wait(barrier, 35)
-
-    @pl.when(jnp.logical_not(sends_beyond))
-    def _():
-        pl.semaphore_wait(barrier, 31)
+    for peers in range(3):
+
+        @pl.when(beyond == peers)
+        def _():
+            pl.semaphore_wait(barrier, 31 + peers)
+
+    first_sends = []
+
+    def reaches(r, ahead):
+        return jnp.logical_and(ahead >= r - 3, ahead <= r + 2)
+
+    def send(copy, sent, sends):
+        sends.append((copy, sent))
+        if sent is True:
+            copy.start()
+        else:
+            pl.when(sent)(copy.start)
+
+    for step in (2, 1, 3, 0):
+        to_y = (y + step) % 4
+        plane = plane_for(to_y)
+        for i in range(2):
+            sent = jnp.logical_and(in_slide(plane), reaches(2 * i, ahead_of(to_y)))
+            if step == 0:
+                mine = jnp.logical_and(sent, plane == z)
+                sent = jnp.logical_and(sent, plane != z)
+
+                @pl.when(mine)
+                def _():
+                    relay_y[i, :, y] = stage_f[2 * i]
+
+            copy = pltpu.make_async_remote_copy(
+                stage_f.at[2 * i], relay_y.at[i, :, y], to_y_send.at[i, step], to_y_sem.at[i, y],
+                device_id=device(2 * plane + core, 4 * to_y + x), device_id_type=MESH,
+            )
+            send(copy, sent, first_sends)
+        to_x = (x + step) % 4
+        for i in range(2):
+            columns = pl.ds(2 * (to_x % 2), WIN_COLS)
+            if step == 0:
+                relay_x[i, :, x] = stage_f[2 * i + 1, columns]
+            else:
+                copy = pltpu.make_async_remote_copy(
+                    stage_f.at[2 * i + 1, columns], relay_x.at[i, :, x],
+                    to_x_send.at[i, step], to_x_sem.at[i, x],
+                    device_id=device(t, 4 * y + to_x), device_id_type=MESH,
+                )
+                send(copy, True, first_sends)
 
     nb_copy = pltpu.make_async_remote_copy(
         nb_own, nb_other, nb_send, nb_sem, device_id=device(partner, f), device_id_type=MESH
@@ -151,34 +205,94 @@
 
     lax.fori_loop(1, 16, start_weight, 0)
 
+    def row_exists(w):
+        row = dest_row + w - 2
+        return jnp.logical_and(row >= 0, row < 4 * n_tiles)
+
+    def clear(w, carry):
+        @pl.when(jnp.logical_not(row_exists(w)))
+        def _():
+            win[w] = jnp.zeros((WIN_COLS, 4, 4, CHUNK, LANES), BF16)
+
+        return carry
+
+    lax.fori_loop(0, WIN_ROWS, clear, 0)
+
+    ones_rows = jnp.ones((16, LANES), BF16)
+
+    def fill_ones(i, carry):
+        feats_t[0, i, pl.ds(LANES, 16)] = ones_rows
+        feats_t[1, i, pl.ds(LANES, 16)] = ones_rows
+        return carry
+
+    lax.fori_loop(0, WIN_ROWS * WIN_COLS, fill_ones, 0)
+
     my_cells = pl.ds(pl.multiple_of(f * CHUNK, CHUNK), CHUNK)
-
-    feat_sends = []
-    for i, chip in enumerate(chips):
-        ahead = jnp.where(core == 0, (chip // 2 + 2) % 8 - 2, (chip // 2 + 6) % 8 - 2)
-        to_row = 4 * t + ahead
-        inside = jnp.logical_and(to_row >= 0, to_row < 4 * n_tiles)
-        tiles = 2 * (to_row // 8) + home
-        for r in range(4):
-            sent = jnp.logical_and(inside, jnp.logical_and(ahead - r >= -2, ahead - r <= 2))
-            if STEPS[i] == (0, 0):
-                sent = jnp.logical_and(sent, tiles != t)
-            w = jnp.clip(r - ahead + 2, 0, WIN_ROWS - 1)
+    second_sends = []
+    ahead = ahead_of(y)
+    band_plane = z + jnp.logical_and(core == 0, y == 3).astype(I32) - jnp.logical_and(
+        core == 1, y == 0).astype(I32)
+
+    for i in range(2):
+        r = 2 * i
+        here = jnp.logical_and(in_slide(band_plane), reaches(r, ahead))
+        for source_y in range(4):
+
+            @pl.when(jnp.logical_and(here, jnp.logical_or(band_plane != z, y != source_y)))
+            def _():
+                pltpu.make_async_copy(
+                    relay_y.at[i, :, source_y], relay_y.at[i, :, source_y], to_y_sem.at[i, source_y]
+                ).wait()
+
+        for step in (2, 1, 3, 0):
+            to_x = (x + step) % 4
+            gap = ahead + to_x // 2 - r
+            w = jnp.clip(2 - gap, 0, WIN_ROWS - 1)
+            columns = pl.ds(2 * (to_x % 2), WIN_COLS)
+            needed = jnp.logical_and(here, jnp.logical_and(gap >= -2, gap <= 2))
+            for q in range(2):
+                sent = needed
+                if step == 0:
+                    sent = jnp.logical_and(needed, core != q)
+
+                    @pl.when(jnp.logical_and(needed, core == q))
+                    def _():
+                        win[w, :, 2 * q : 2 * q + 2, x] = relay_y[i, columns, 2 * q : 2 * q + 2]
+
+                copy = pltpu.make_async_remote_copy(
+                    relay_y.at[i, columns, pl.ds(2 * q, 2)], win.at[w, :, pl.ds(2 * q, 2), x],
+                    win_y_send.at[i, step, q], win_y_sem.at[w, x],
+                    device_id=device(2 * z + q, 4 * y + to_x), device_id_type=MESH,
+                )
+                send(copy, sent, second_sends)
+
+        r = 2 * i + 1
+        for step in range(1, 4):
+            source_x = (x + step) % 4
+            pltpu.make_async_copy(
+                relay_x.at[i, :, source_x], relay_x.at[i, :, source_x], to_x_sem.at[i, source_x]
+            ).wait()
+
+        for step in (2, 1, 3, 0):
+            to_y = (y + step) % 4
+            plane = plane_for(to_y)
+            gap = ahead_of(to_y) + x // 2 - r
+            w = jnp.clip(2 - gap, 0, WIN_ROWS - 1)
+            sent = jnp.logical_and(in_slide(plane), jnp.logical_and(gap >= -2, gap <= 2))
+            if step == 0:
+                at_home = jnp.logical_and(plane == z, home == core)
+                mine = jnp.logical_and(sent, at_home)
+                sent = jnp.logical_and(sent, jnp.logical_not(at_home))
+
+                @pl.when(mine)
+                def _():
+                    win[w, :, y] = relay_x[i]
+
             copy = pltpu.make_async_remote_copy(
-                stage_f.at[r, pl.ds(2 * (chip % 2), WIN_COLS)],
-                win.at[w, :, my_cells],
-                win_send.at[4 * i + r], win_sem.at[w, f % 8],
-                device_id=device(tiles, chip), device_id_type=MESH,
+                relay_x.at[i], win.at[w, :, y], win_x_send.at[i, step], win_x_sem.at[w, y % 2],
+                device_id=device(2 * plane + home, 4 * to_y + x), device_id_type=MESH,
             )
-            feat_sends.append((copy, sent))
-            pl.when(sent)(copy.start)
-
-    for r in range(4):
-        w = 4 * t + r - dest_row + 2
-
-        @pl.when(jnp.logical_and(home == core, jnp.logical_and(w >= 0, w < WIN_ROWS)))
-        def _():
-            win[w, :, my_cells] = stage_f[r, pl.ds(2 * half, WIN_COLS)]
+            send(copy, sent, second_sends)
 
     def invert(r, carry):
         found = 0
@@ -188,28 +302,6 @@
         return carry
 
     lax.fori_loop(0, TILES, invert, 0)
-
-    def row_exists(w):
-        row = dest_row + w - 2
-        return jnp.logical_and(row >= 0, row < 4 * n_tiles)
-
-    def clear(w, carry):
-        @pl.when(jnp.logical_not(row_exists(w)))
-        def _():
-            win[w] = jnp.zeros((WIN_COLS, CELLS, LANES), BF16)
-
-        return carry
-
-    lax.fori_loop(0, WIN_ROWS, clear, 0)
-
-    ones_rows = jnp.ones((16, LANES), BF16)
-
-    def fill_ones(i, carry):
-        feats_t[0, i, pl.ds(LANES, 16)] = ones_rows
-        feats_t[1, i, pl.ds(LANES, 16)] = ones_rows
-        return carry
-
-    lax.fori_loop(0, WIN_ROWS * WIN_COLS, fill_ones, 0)
 
     def unpack(k, carry):
         @pl.when(jnp.logical_not(jnp.logical_and(k == f, core == home)))
@@ -235,7 +327,7 @@
         return carry
 
     lax.fori_loop(1, 16, weight_wait, 0)
-    kept = pl.ds(pl.multiple_of(core * LANES, LANES), LANES)
+    kept = pl.ds(2 * core, 2)
 
     def forward_copy(w):
         return pltpu.make_async_remote_copy(
@@ -244,32 +336,41 @@
         )
 
     def forward(w, carry):
+        from_here = (dest_row + w - 2) // 4 == t
+        from_chip = (dest_row + w - 2) // 4 % 2 == core
+        even = (dest_row + w) % 2 == 0
+
+        @pl.when(jnp.logical_and(row_exists(w), even))
+        def _():
+            for source_x in range(4):
+
+                @pl.when(jnp.logical_not(jnp.logical_and(from_chip, x == source_x)))
+                def _():
+                    piece = win.at[w, :, kept, source_x]
+                    pltpu.make_async_copy(piece, piece, win_y_sem.at[w, source_x]).wait()
+
+        @pl.when(jnp.logical_and(row_exists(w), jnp.logical_not(even)))
+        def _():
+            for side in range(2):
+
+                @pl.when(jnp.logical_not(jnp.logical_and(from_here, y == 2 * core + side)))
+                def _():
+                    piece = win.at[w, :, 2 * core + side]
+                    pltpu.make_async_copy(piece, piece, win_x_sem.at[w, side]).wait()
+
         @pl.when(row_exists(w))
         def _():
-            local = jnp.logical_and(home == core, (dest_row + w - 2) // 4 == t)
-
-            def arrive(i, c):
-                @pl.when(jnp.logical_not(jnp.logical_and(local, i == f % 8)))
-                def _():
-                    cells = pl.ds(pl.multiple_of((core * 8 + i) * CHUNK, CHUNK), CHUNK)
-                    pltpu.make_async_copy(
-                        win.at[w, :, cells], win.at[w, :, cells], win_sem.at[w, i]
-                    ).wait()
-
-                return c
-
-            lax.fori_loop(0, 8, arrive, 0)
             forward_copy(w).start()
 
         return carry
 
     lax.fori_loop(0, WIN_ROWS, forward, 0)
 
-    given = pl.ds(pl.multiple_of((1 - core) * LANES, LANES), LANES)
+    given = pl.ds(2 - 2 * core, 2)
 
     def turn_kept(w, carry):
         for c in range(WIN_COLS):
-            feats_t[core, w * WIN_COLS + c, pl.ds(0, LANES)] = win[w, c, kept].T
+            feats_t[core, w * WIN_COLS + c, pl.ds(0, LANES)] = win[w, c, kept].reshape(LANES, LANES).T
         return carry
 
     lax.fori_loop(0, WIN_ROWS, turn_kept, 0)
@@ -280,7 +381,7 @@
             forward_copy(w).wait_recv()
 
         for c in range(WIN_COLS):
-            feats_t[1 - core, w * WIN_COLS + c, pl.ds(0, LANES)] = win[w, c, given].T
+            feats_t[1 - core, w * WIN_COLS + c, pl.ds(0, LANES)] = win[w, c, given].reshape(LANES, LANES).T
         return carry
 
     lax.fori_loop(0, WIN_ROWS, turn_given, 0)
@@ -310,7 +411,7 @@
     totals = lax.fori_loop(0, SLOTS, add, (zero, zero), unroll=True)
     for tile in range(2):
         total = totals[tile].T
-        base = win[2, 4 * half + 2 * core + tile - 2 * half].astype(F32)
+        base = win[2, 4 * half + 2 * core + tile - 2 * half].reshape(CELLS, LANES).astype(F32)
         degree = total[:, LANES : LANES + 1]
         normed = ((total[:, :LANES] + base) / jnp.sqrt(degree + 1.0)).astype(BF16)
         linear = jnp.dot(normed, weight, preferred_element_type=F32) + bias
@@ -348,8 +449,11 @@
 
     lax.fori_loop(1, 16, end_weight, 0)
 
-    for copy, sent in feat_sends:
-        pl.when(sent)(copy.wait_send)
+    for copy, sent in first_sends + second_sends:
+        if sent is True:
+            copy.wait_send()
+        else:
+            pl.when(sent)(copy.wait_send)
 
     def end_forward(w, carry):
         @pl.when(row_exists(w))
@@ -406,7 +510,9 @@
                 pltpu.SMEM((SLOTS, TILES), I32),
                 pltpu.VMEM((4, 8, CHUNK, LANES), BF16),
                 pltpu.VMEM((TILES, WORDS, LANES), I32),
-                pltpu.VMEM((WIN_ROWS, WIN_COLS, CELLS, LANES), BF16),
+                pltpu.VMEM((2, 8, 4, CHUNK, LANES), BF16),
+                pltpu.VMEM((2, WIN_COLS, 4, CHUNK, LANES), BF16),
+                pltpu.VMEM((WIN_ROWS, WIN_COLS, 4, 4, CHUNK, LANES), BF16),
                 pltpu.VMEM((SLOTS, 2, WORDS, LANES), I32),
                 pltpu.VMEM((16, 8, LANES), BF16),
                 pltpu.VMEM((2, WORDS * BITS, LANES), I32),
@@ -422,8 +528,14 @@
                 pltpu.SemaphoreType.DMA((SLOTS,)),
                 pltpu.SemaphoreType.DMA((16,)),
                 pltpu.SemaphoreType.DMA((16,)),
-                pltpu.SemaphoreType.DMA((64,)),
-                pltpu.SemaphoreType.DMA((WIN_ROWS, 8)),
+                pltpu.SemaphoreType.DMA((2, 4)),
+                pltpu.SemaphoreType.DMA((2, 4)),
+                pltpu.SemaphoreType.DMA((2, 4)),
+                pltpu.SemaphoreType.DMA((2, 4)),
+                pltpu.SemaphoreType.DMA((2, 4, 2)),
+                pltpu.SemaphoreType.DMA((WIN_ROWS, 4)),
+                pltpu.SemaphoreType.DMA((2, 4)),
+                pltpu.SemaphoreType.DMA((WIN_ROWS, 2)),
                 pltpu.SemaphoreType.DMA((WIN_ROWS,)),
                 pltpu.SemaphoreType.DMA((WIN_ROWS,)),
                 pltpu.SemaphoreType.DMA((16,)),

time: 39 us -> 36.7 us (0.941)
  Pallas kernels: 38.2 us -> 35.9 us
    pallas_call x1, Pallas kernels: 38.2 us -> 35.9 us  [per_device(): pl.pallas_call(functools.partial(kernel, n_tiles), out_shape=pltpu.VMEM(f...]
where the time goes in v4:
time: 36.7 us; the launch traced here: 36.6 us
  Pallas kernels  35.9 us (98%)
  local copies, waits for them, and re-layouts  0.66 us (2%)
    pallas_call x1, Pallas kernels, per_device(): pl.pallas_call(functools.partial(kernel, n_tiles), out_shape=pltpu.VMEM(f...  35.9 us

profile of v4, /device:TPU:1, one launch (start us, length us, event | category | flops | bytes accessed | tf_op | source)
XLA Modules:
  0.0 36.6 jit_solution(9510274145177337037)
XLA Ops:
  0.0 35.9 %shard_map.73 = bf16[32,16,128]{2,1,0:T(8,128)(2,1)S(1)} custom-call(bf16[32,16,128]{2,1,0:T(8,128)(2,1)} %feats_hbm.1, bf16[8,128]{1,0:T(8,128)(2,1)} %weight_hbm.1, f32[1,128]{1,0:T(1,128)} %bitcast.5, s32[16,32]{1,0:T(8,128)} %bitcast.4, s32[32,24,256]{2,1,0:T(8,128)} %bitcast.3, s32[32]{0:T(128)} %counts_hbm.1, s32[1024]{0:T(1024)} %rows_hbm.1), custom_call_target="tpu_custom_call" | custom-call | tf_op jit(solution)/shard_map/pallas_call | solution.py:497
  35.9 0.7 %copy.9 = bf16[32,16,128]{2,1,0:T(8,128)(2,1)} copy(bf16[32,16,128]{2,1,0:T(8,128)(2,1)S(1)} %shard_map.73) | data formatting | bytes 262144

commit v5 on v4

--- a/solution.py
+++ b/solution.py
@@ -32,7 +32,7 @@
     feats_hbm, weight_hbm, bias_hbm, nb_hbm, words_hbm, counts_hbm, rows_hbm,
     out_ref,
     feats_v, words_v, weight_v, bias_ref, counts_ref, rows_ref, nb_own, nb_other, stage_f, stage_w, relay_y, relay_x, win, wbuf, wall, bits32, mask, feats_t, stage_o, obuf, inverse,
-    local_sem, nb_send, nb_sem, word_send, word_sem, weight_send, weight_sem, to_y_send, to_y_sem, to_x_send, to_x_sem, win_y_send, win_y_sem, win_x_send, win_x_sem, fwd_send, fwd_sem, out_send, out_sem,
+    local_sem, nb_send, nb_sem, word_send, word_sem, weight_send, weight_sem, to_y_send, to_y_sem, to_x_send, to_x_sem, win_y_send, win_x_send, win_sem, fwd_send, fwd_sem, out_send, out_sem,
 ):
     t = lax.axis_index("tiles")
     f = lax.axis_index("feat")
@@ -49,6 +49,17 @@
     def device(tiles, feat):
         return {"tiles": tiles, "feat": feat}
 
+    def settle(sem, piece):
+        pltpu.make_async_copy(piece, piece, sem).wait()
+
+    def settle_count(sem, sent, most, pieces):
+        count = sum(jnp.asarray(one).astype(I32) for one in sent)
+        for n in range(1, most + 1):
+
+            @pl.when(count == n)
+            def _():
+                settle(sem, pieces(n))
+
     loads = [
         pltpu.make_async_copy(words_hbm, words_v, local_sem.at[0]),
         pltpu.make_async_copy(feats_hbm, feats_v, local_sem.at[1]),
@@ -123,13 +134,13 @@
         def _():
             pl.semaphore_wait(barrier, 31 + peers)
 
-    first_sends = []
+    first_y, first_x, second_y, second_x = ([], []), [], [], []
 
     def reaches(r, ahead):
         return jnp.logical_and(ahead >= r - 3, ahead <= r + 2)
 
     def send(copy, sent, sends):
-        sends.append((copy, sent))
+        sends.append(sent)
         if sent is True:
             copy.start()
         else:
@@ -149,10 +160,10 @@
                     relay_y[i, :, y] = stage_f[2 * i]
 
             copy = pltpu.make_async_remote_copy(
-                stage_f.at[2 * i], relay_y.at[i, :, y], to_y_send.at[i, step], to_y_sem.at[i, y],
+                stage_f.at[2 * i], relay_y.at[i, :, y], to_y_send.at[i], to_y_sem.at[i],
                 device_id=device(2 * plane + core, 4 * to_y + x), device_id_type=MESH,
             )
-            send(copy, sent, first_sends)
+            send(copy, sent, first_y[i])
         to_x = (x + step) % 4
         for i in range(2):
             columns = pl.ds(2 * (to_x % 2), WIN_COLS)
@@ -161,10 +172,10 @@
             else:
                 copy = pltpu.make_async_remote_copy(
                     stage_f.at[2 * i + 1, columns], relay_x.at[i, :, x],
-                    to_x_send.at[i, step], to_x_sem.at[i, x],
+                    to_x_send, to_x_sem.at[i],
                     device_id=device(t, 4 * y + to_x), device_id_type=MESH,
                 )
-                send(copy, True, first_sends)
+                send(copy, True, first_x)
 
     nb_copy = pltpu.make_async_remote_copy(
         nb_own, nb_other, nb_send, nb_sem, device_id=device(partner, f), device_id_type=MESH
@@ -179,10 +190,10 @@
                 sent = jnp.logical_and(sent, side != core)
             copy = pltpu.make_async_remote_copy(
                 stage_w.at[pl.ds(4 * (chip % 8) + 2 * side, 2)], wbuf.at[f],
-                word_send.at[2 * i + side], word_sem.at[f],
+                word_send, word_sem.at[f // 4],
                 device_id=device(2 * z + side, chip), device_id_type=MESH,
             )
-            word_sends.append((copy, sent))
+            word_sends.append(sent)
             pl.when(sent)(copy.start)
 
     @pl.when(home == core)
@@ -195,7 +206,7 @@
     def weight_copy(i):
         chip = (f + i) % 16
         return pltpu.make_async_remote_copy(
-            weight_v, wall.at[f], weight_send.at[i], weight_sem.at[f],
+            weight_v, wall.at[f], weight_send, weight_sem,
             device_id=device(t, chip), device_id_type=MESH,
         )
 
@@ -228,7 +239,6 @@
     lax.fori_loop(0, WIN_ROWS * WIN_COLS, fill_ones, 0)
 
     my_cells = pl.ds(pl.multiple_of(f * CHUNK, CHUNK), CHUNK)
-    second_sends = []
     ahead = ahead_of(y)
     band_plane = z + jnp.logical_and(core == 0, y == 3).astype(I32) - jnp.logical_and(
         core == 1, y == 0).astype(I32)
@@ -236,13 +246,14 @@
     for i in range(2):
         r = 2 * i
         here = jnp.logical_and(in_slide(band_plane), reaches(r, ahead))
-        for source_y in range(4):
-
-            @pl.when(jnp.logical_and(here, jnp.logical_or(band_plane != z, y != source_y)))
-            def _():
-                pltpu.make_async_copy(
-                    relay_y.at[i, :, source_y], relay_y.at[i, :, source_y], to_y_sem.at[i, source_y]
-                ).wait()
+
+        @pl.when(jnp.logical_and(here, band_plane != z))
+        def _():
+            settle(to_y_sem.at[i], relay_y.at[i])
+
+        @pl.when(jnp.logical_and(here, band_plane == z))
+        def _():
+            settle(to_y_sem.at[i], relay_y.at[i, :, pl.ds(0, 3)])
 
         for step in (2, 1, 3, 0):
             to_x = (x + step) % 4
@@ -261,17 +272,13 @@
 
                 copy = pltpu.make_async_remote_copy(
                     relay_y.at[i, columns, pl.ds(2 * q, 2)], win.at[w, :, pl.ds(2 * q, 2), x],
-                    win_y_send.at[i, step, q], win_y_sem.at[w, x],
+                    win_y_send, win_sem.at[w],
                     device_id=device(2 * z + q, 4 * y + to_x), device_id_type=MESH,
                 )
-                send(copy, sent, second_sends)
+                send(copy, sent, second_y)
 
         r = 2 * i + 1
-        for step in range(1, 4):
-            source_x = (x + step) % 4
-            pltpu.make_async_copy(
-                relay_x.at[i, :, source_x], relay_x.at[i, :, source_x], to_x_sem.at[i, source_x]
-            ).wait()
+        settle(to_x_sem.at[i], relay_x.at[i, :, pl.ds(0, 3)])
 
         for step in (2, 1, 3, 0):
             to_y = (y + step) % 4
@@ -289,10 +296,10 @@
                     win[w, :, y] = relay_x[i]
 
             copy = pltpu.make_async_remote_copy(
-                relay_x.at[i], win.at[w, :, y], win_x_send.at[i, step], win_x_sem.at[w, y % 2],
+                relay_x.at[i], win.at[w, :, y], win_x_send, win_sem.at[w],
                 device_id=device(2 * plane + home, 4 * to_y + x), device_id_type=MESH,
             )
-            send(copy, sent, second_sends)
+            send(copy, sent, second_x)
 
     def invert(r, carry):
         found = 0
@@ -304,9 +311,15 @@
     lax.fori_loop(0, TILES, invert, 0)
 
     def unpack(k, carry):
-        @pl.when(jnp.logical_not(jnp.logical_and(k == f, core == home)))
-        def _():
-            pltpu.make_async_copy(wbuf.at[k], wbuf.at[k], word_sem.at[k]).wait()
+        with_mine = jnp.logical_and(k == f // 4 * 4, core == home)
+
+        @pl.when(with_mine)
+        def _():
+            settle(word_sem.at[k // 4], wbuf.at[pl.ds(k, 3)])
+
+        @pl.when(jnp.logical_and(k % 4 == 0, jnp.logical_not(with_mine)))
+        def _():
+            settle(word_sem.at[k // 4], wbuf.at[pl.ds(k, 4)])
 
         for tile in range(2):
             packed = wbuf[k, tile]
@@ -321,17 +334,12 @@
 
     nb_copy.wait_recv()
 
-    def weight_wait(i, carry):
-        chip = (f + i) % 16
-        pltpu.make_async_copy(wall.at[chip], wall.at[chip], weight_sem.at[chip]).wait()
-        return carry
-
-    lax.fori_loop(1, 16, weight_wait, 0)
+    settle(weight_sem, wall.at[pl.ds(0, 15)])
     kept = pl.ds(2 * core, 2)
 
     def forward_copy(w):
         return pltpu.make_async_remote_copy(
-            win.at[w, :, kept], win.at[w, :, kept], fwd_send.at[w], fwd_sem.at[w],
+            win.at[w, :, kept], win.at[w, :, kept], fwd_send, fwd_sem.at[w],
             device_id=device(partner, f), device_id_type=MESH,
         )
 
@@ -340,23 +348,19 @@
         from_chip = (dest_row + w - 2) // 4 % 2 == core
         even = (dest_row + w) % 2 == 0
 
-        @pl.when(jnp.logical_and(row_exists(w), even))
-        def _():
-            for source_x in range(4):
-
-                @pl.when(jnp.logical_not(jnp.logical_and(from_chip, x == source_x)))
-                def _():
-                    piece = win.at[w, :, kept, source_x]
-                    pltpu.make_async_copy(piece, piece, win_y_sem.at[w, source_x]).wait()
-
-        @pl.when(jnp.logical_and(row_exists(w), jnp.logical_not(even)))
-        def _():
-            for side in range(2):
-
-                @pl.when(jnp.logical_not(jnp.logical_and(from_here, y == 2 * core + side)))
-                def _():
-                    piece = win.at[w, :, 2 * core + side]
-                    pltpu.make_async_copy(piece, piece, win_x_sem.at[w, side]).wait()
+        part_here = jnp.where(even, from_chip, jnp.logical_and(from_here, home == core))
+
+        @pl.when(jnp.logical_and(row_exists(w), jnp.logical_not(part_here)))
+        def _():
+            settle(win_sem.at[w], win.at[w, :, kept])
+
+        @pl.when(jnp.logical_and(row_exists(w), jnp.logical_and(part_here, even)))
+        def _():
+            settle(win_sem.at[w], win.at[w, :, kept, pl.ds(0, 3)])
+
+        @pl.when(jnp.logical_and(row_exists(w), jnp.logical_and(part_here, jnp.logical_not(even))))
+        def _():
+            settle(win_sem.at[w], win.at[w, :, 2 * core])
 
         @pl.when(row_exists(w))
         def _():
@@ -419,16 +423,14 @@
 
     first_out = 4 * (f % 8) + 2 * core
 
-    out_sends = []
     for i, chip in enumerate(chips):
         cells = pl.ds(pl.multiple_of(chip * CHUNK, CHUNK), CHUNK)
         copy = pltpu.make_async_remote_copy(
             stage_o.at[:, cells], obuf.at[pl.ds(first_out, 2)],
-            out_send.at[i], out_sem.at[first_out // 2],
+            out_send, out_sem,
             device_id=device(2 * z + home, chip), device_id_type=MESH,
         )
         sent = home != core if STEPS[i] == (0, 0) else True
-        out_sends.append((copy, sent))
         if sent is True:
             copy.start()
         else:
@@ -439,46 +441,33 @@
         obuf[pl.ds(first_out, 2)] = stage_o[:, my_cells]
 
     nb_copy.wait_send()
-
-    for copy, sent in word_sends:
-        pl.when(sent)(copy.wait_send)
-
-    def end_weight(i, carry):
-        weight_copy(i).wait_send()
-        return carry
-
-    lax.fori_loop(1, 16, end_weight, 0)
-
-    for copy, sent in first_sends + second_sends:
-        if sent is True:
-            copy.wait_send()
-        else:
-            pl.when(sent)(copy.wait_send)
-
-    def end_forward(w, carry):
-        @pl.when(row_exists(w))
-        def _():
-            forward_copy(w).wait_send()
-
-        return carry
-
-    lax.fori_loop(0, WIN_ROWS, end_forward, 0)
-
-    for copy, sent in out_sends:
-        if sent is True:
-            copy.wait_send()
-        else:
-            pl.when(sent)(copy.wait_send)
-
-    def arrive_out(i, carry):
-        @pl.when(jnp.logical_not(jnp.logical_and(home == core, i == first_out // 2)))
-        def _():
-            pair = pl.ds(2 * i, 2)
-            pltpu.make_async_copy(obuf.at[pair], obuf.at[pair], out_sem.at[i]).wait()
-
-        return carry
-
-    lax.fori_loop(0, 16, arrive_out, 0)
+    settle(weight_send, wall.at[pl.ds(0, 15)])
+    for i in range(2):
+        settle_count(to_y_send.at[i], first_y[i], 3, lambda n: relay_y.at[0, :, pl.ds(0, n)])
+    settle(to_x_send, relay_x.at[:, :, pl.ds(0, 3)])
+    settle_count(win_y_send, second_y, 16, lambda n: words_v.at[pl.ds(0, 2 * n)])
+    settle_count(win_x_send, second_x, 8, lambda n: words_v.at[pl.ds(0, 4 * n)])
+    settle_count(
+        fwd_send, [row_exists(w) for w in range(WIN_ROWS)], WIN_ROWS, lambda n: win.at[pl.ds(0, n), :, kept]
+    )
+
+    @pl.when(home == core)
+    def _():
+        settle(word_send, stage_w.at[pl.ds(0, 30)])
+        settle(out_send, obuf.at[pl.ds(0, 30)])
+
+    @pl.when(home != core)
+    def _():
+        settle(word_send, stage_w)
+        settle(out_send, obuf)
+
+    @pl.when(home == core)
+    def _():
+        settle(out_sem, obuf.at[pl.ds(0, 30)])
+
+    @pl.when(home != core)
+    def _():
+        settle(out_sem, obuf)
 
     def put(r, carry):
         out_ref[r] = obuf[inverse[r]]
@@ -524,22 +513,21 @@
                 pltpu.SemaphoreType.DMA((7,)),
                 pltpu.SemaphoreType.DMA,
                 pltpu.SemaphoreType.DMA,
-                pltpu.SemaphoreType.DMA((32,)),
-                pltpu.SemaphoreType.DMA((SLOTS,)),
-                pltpu.SemaphoreType.DMA((16,)),
-                pltpu.SemaphoreType.DMA((16,)),
-                pltpu.SemaphoreType.DMA((2, 4)),
-                pltpu.SemaphoreType.DMA((2, 4)),
-                pltpu.SemaphoreType.DMA((2, 4)),
-                pltpu.SemaphoreType.DMA((2, 4)),
-                pltpu.SemaphoreType.DMA((2, 4, 2)),
-                pltpu.SemaphoreType.DMA((WIN_ROWS, 4)),
-                pltpu.SemaphoreType.DMA((2, 4)),
-                pltpu.SemaphoreType.DMA((WIN_ROWS, 2)),
+                pltpu.SemaphoreType.DMA,
+                pltpu.SemaphoreType.DMA((4,)),
+                pltpu.SemaphoreType.DMA,
+                pltpu.SemaphoreType.DMA,
+                pltpu.SemaphoreType.DMA((2,)),
+                pltpu.SemaphoreType.DMA((2,)),
+                pltpu.SemaphoreType.DMA,
+                pltpu.SemaphoreType.DMA((2,)),
+                pltpu.SemaphoreType.DMA,
+                pltpu.SemaphoreType.DMA,
                 pltpu.SemaphoreType.DMA((WIN_ROWS,)),
+                pltpu.SemaphoreType.DMA,
                 pltpu.SemaphoreType.DMA((WIN_ROWS,)),
-                pltpu.SemaphoreType.DMA((16,)),
-                pltpu.SemaphoreType.DMA((16,)),
+                pltpu.SemaphoreType.DMA,
+                pltpu.SemaphoreType.DMA,
             ],
             compiler_params=pltpu.CompilerParams(collective_id=0, has_side_effects=True),
         )(feats, weight, bias.reshape(1, LANES), neighbours.T, words, counts, tile_row)

time: 36.7 us -> 35.1 us (0.956)
  Pallas kernels: 35.9 us -> 34.3 us
    pallas_call x1, Pallas kernels: 35.9 us -> 34.3 us  [per_device(): pl.pallas_call(functools.partial(kernel, n_tiles), out_shape=pltpu.VMEM(f...]
where the time goes in v5:
time: 35.1 us; the launch traced here: 34.9 us
  Pallas kernels  34.3 us (98%)
  local copies, waits for them, and re-layouts  0.66 us (2%)
    pallas_call x1, Pallas kernels, per_device(): pl.pallas_call(functools.partial(kernel, n_tiles), out_shape=pltpu.VMEM(f...  34.3 us

profile of v5, /device:TPU:1, one launch (start us, length us, event | category | flops | bytes accessed | tf_op | source)
XLA Modules:
  0.0 34.9 jit_solution(3051111049108013566)
XLA Ops:
  0.0 34.3 %shard_map.73 = bf16[32,16,128]{2,1,0:T(8,128)(2,1)S(1)} custom-call(bf16[32,16,128]{2,1,0:T(8,128)(2,1)} %feats_hbm.1, bf16[8,128]{1,0:T(8,128)(2,1)} %weight_hbm.1, f32[1,128]{1,0:T(1,128)} %bitcast.5, s32[16,32]{1,0:T(8,128)} %bitcast.4, s32[32,24,256]{2,1,0:T(8,128)} %bitcast.3, s32[32]{0:T(128)} %counts_hbm.1, s32[1024]{0:T(1024)} %rows_hbm.1), custom_call_target="tpu_custom_call" | custom-call | tf_op jit(solution)/shard_map/pallas_call | solution.py:486
  34.3 0.7 %copy.9 = bf16[32,16,128]{2,1,0:T(8,128)(2,1)} copy(bf16[32,16,128]{2,1,0:T(8,128)(2,1)S(1)} %shard_map.73) | data formatting | bytes 262144

commit v6 on v5

--- a/solution.py
+++ b/solution.py
@@ -32,7 +32,7 @@
     feats_hbm, weight_hbm, bias_hbm, nb_hbm, words_hbm, counts_hbm, rows_hbm,
     out_ref,
     feats_v, words_v, weight_v, bias_ref, counts_ref, rows_ref, nb_own, nb_other, stage_f, stage_w, relay_y, relay_x, win, wbuf, wall, bits32, mask, feats_t, stage_o, obuf, inverse,
-    local_sem, nb_send, nb_sem, word_send, word_sem, weight_send, weight_sem, to_y_send, to_y_sem, to_x_send, to_x_sem, win_y_send, win_x_send, win_sem, fwd_send, fwd_sem, out_send, out_sem,
+    local_sem, met_sem, nb_send, nb_sem, word_send, word_sem, weight_send, weight_sem, to_y_send, to_y_sem, to_x_send, to_x_sem, win_y_send, win_x_send, win_sem, fwd_send, fwd_sem, out_send, out_sem,
 ):
     t = lax.axis_index("tiles")
     f = lax.axis_index("feat")
@@ -60,25 +60,39 @@
             def _():
                 settle(sem, pieces(n))
 
-    loads = [
-        pltpu.make_async_copy(words_hbm, words_v, local_sem.at[0]),
+    early = [
+        pltpu.make_async_copy(rows_hbm, rows_ref, local_sem.at[0]),
         pltpu.make_async_copy(feats_hbm, feats_v, local_sem.at[1]),
-        pltpu.make_async_copy(weight_hbm, weight_v, local_sem.at[2]),
-        pltpu.make_async_copy(nb_hbm, nb_own, local_sem.at[3]),
-        pltpu.make_async_copy(bias_hbm, bias_ref, local_sem.at[4]),
-        pltpu.make_async_copy(counts_hbm, counts_ref, local_sem.at[5]),
-        pltpu.make_async_copy(rows_hbm, rows_ref, local_sem.at[6]),
     ]
-    for load in loads:
+    late = [
+        pltpu.make_async_copy(words_hbm, words_v, local_sem.at[2]),
+        pltpu.make_async_copy(counts_hbm, counts_ref, local_sem.at[3]),
+        pltpu.make_async_copy(nb_hbm, nb_own, local_sem.at[4]),
+        pltpu.make_async_copy(weight_hbm, weight_v, local_sem.at[5]),
+        pltpu.make_async_copy(bias_hbm, bias_ref, local_sem.at[6]),
+    ]
+    for load in early:
         load.start()
 
     barrier = pltpu.get_barrier_semaphore()
 
     chips = [(f // 4 + dy) % 4 * 4 + (f % 4 + dx) % 4 for dy, dx in STEPS]
 
-    for i, chip in enumerate(chips):
-        for tiles in (partner,) if STEPS[i] == (0, 0) else (t, partner):
-            pl.semaphore_signal(barrier, inc=1, device_id=device(tiles, chip), device_id_type=MESH)
+    for (dy, dx), chip in zip(STEPS, chips):
+        if dy * dx == 0:
+            for tiles in (partner,) if (dy, dx) == (0, 0) else (t, partner):
+                pl.semaphore_signal(barrier, inc=1, device_id=device(tiles, chip), device_id_type=MESH)
+
+    @pl.when(z > 0)
+    def _():
+        pl.semaphore_signal(barrier, inc=1, device_id=device(t - 2, f), device_id_type=MESH)
+
+    @pl.when(z < n_planes - 1)
+    def _():
+        pl.semaphore_signal(barrier, inc=1, device_id=device(t + 2, f), device_id_type=MESH)
+
+    for load in late:
+        load.start()
 
     def plane_for(chip_y):
         below = jnp.logical_and(core == 0, chip_y == 3).astype(I32)
@@ -91,48 +105,37 @@
     def in_slide(plane):
         return jnp.logical_and(plane >= 0, plane < n_planes)
 
-    for source_y in range(4):
-        above = jnp.logical_and(y == 3, z < n_planes - 1)
-        below = jnp.logical_and(y == 0, z > 0)
-        if source_y < 2:
-            above = jnp.logical_and(above, core == 0)
-        else:
-            below = jnp.logical_and(below, core == 1)
-
-        @pl.when(above)
-        def _():
-            pl.semaphore_signal(
-                barrier, inc=1, device_id=device(2 * z + 2, 4 * source_y + x), device_id_type=MESH
-            )
-
-        @pl.when(below)
-        def _():
-            pl.semaphore_signal(
-                barrier, inc=1, device_id=device(2 * z - 1, 4 * source_y + x), device_id_type=MESH
-            )
-
-    for load in loads:
+    for load in early:
         load.wait()
 
-    def order(s, carry):
-        row = jnp.clip(rows_ref[t * TILES + s] - t * TILES, 0, TILES - 1)
-        live = f < counts_ref[row]
-        w = words_v[row]
-        packed = w[:, :LANES] | (w[:, LANES:] << 16)
-        stage_w[s] = jnp.where(live, packed, jnp.zeros_like(packed))
-        stage_f[s // 8, s % 8] = feats_v[row]
-        return carry
-
-    lax.fori_loop(0, TILES, order, 0)
-
-    beyond = jnp.where(
-        core == 0, jnp.where(z > 0, 1 + y // 2, 0), jnp.where(z < n_planes - 1, 2 - y // 2, 0)
-    )
-    for peers in range(3):
-
-        @pl.when(beyond == peers)
-        def _():
-            pl.semaphore_wait(barrier, 31 + peers)
+    def own_row(s):
+        return jnp.clip(rows_ref[t * TILES + s] - t * TILES, 0, TILES - 1)
+
+    for s in range(TILES):
+        stage_f[s // 8, s % 8] = feats_v[own_row(s)]
+
+    at_end = jnp.logical_or(z == 0, z == n_planes - 1)
+
+    @pl.when(at_end)
+    def _():
+        pl.semaphore_wait(barrier, 14)
+
+    @pl.when(jnp.logical_not(at_end))
+    def _():
+        pl.semaphore_wait(barrier, 15)
+
+    for step in (2, 1, 3):
+        pl.semaphore_signal(
+            met_sem, inc=1, device_id=device(t, (y + step) % 4 * 4 + x), device_id_type=MESH
+        )
+
+    @pl.when(jnp.logical_and(core == 0, z < n_planes - 1))
+    def _():
+        pl.semaphore_signal(met_sem, inc=1, device_id=device(t + 2, f), device_id_type=MESH)
+
+    @pl.when(jnp.logical_and(core == 1, z > 0))
+    def _():
+        pl.semaphore_signal(met_sem, inc=1, device_id=device(t - 2, f), device_id_type=MESH)
 
     first_y, first_x, second_y, second_x = ([], []), [], [], []
 
@@ -146,24 +149,27 @@
         else:
             pl.when(sent)(copy.start)
 
-    for step in (2, 1, 3, 0):
+    def first_along_y(step, i, in_plane):
         to_y = (y + step) % 4
         plane = plane_for(to_y)
+        sent = jnp.logical_and(in_slide(plane), reaches(2 * i, ahead_of(to_y)))
+        sent = jnp.logical_and(sent, (plane == z) == in_plane)
+        if in_plane and step == 0:
+
+            @pl.when(sent)
+            def _():
+                relay_y[i, :, y] = stage_f[2 * i]
+
+            return
+        copy = pltpu.make_async_remote_copy(
+            stage_f.at[2 * i], relay_y.at[i, :, y], to_y_send.at[i], to_y_sem.at[i],
+            device_id=device(2 * plane + core, 4 * to_y + x), device_id_type=MESH,
+        )
+        send(copy, sent, first_y[i])
+
+    for step in (2, 1, 3, 0):
         for i in range(2):
-            sent = jnp.logical_and(in_slide(plane), reaches(2 * i, ahead_of(to_y)))
-            if step == 0:
-                mine = jnp.logical_and(sent, plane == z)
-                sent = jnp.logical_and(sent, plane != z)
-
-                @pl.when(mine)
-                def _():
-                    relay_y[i, :, y] = stage_f[2 * i]
-
-            copy = pltpu.make_async_remote_copy(
-                stage_f.at[2 * i], relay_y.at[i, :, y], to_y_send.at[i], to_y_sem.at[i],
-                device_id=device(2 * plane + core, 4 * to_y + x), device_id_type=MESH,
-            )
-            send(copy, sent, first_y[i])
+            first_along_y(step, i, True)
         to_x = (x + step) % 4
         for i in range(2):
             columns = pl.ds(2 * (to_x % 2), WIN_COLS)
@@ -176,6 +182,33 @@
                     device_id=device(t, 4 * y + to_x), device_id_type=MESH,
                 )
                 send(copy, True, first_x)
+
+    for load in late:
+        load.wait()
+
+    def order_words(s, carry):
+        row = own_row(s)
+        live = f < counts_ref[row]
+        w = words_v[row]
+        packed = w[:, :LANES] | (w[:, LANES:] << 16)
+        stage_w[s] = jnp.where(live, packed, jnp.zeros_like(packed))
+        return carry
+
+    lax.fori_loop(0, TILES, order_words, 0)
+
+    meets_beyond = jnp.where(core == 0, z > 0, z < n_planes - 1)
+
+    @pl.when(meets_beyond)
+    def _():
+        pl.semaphore_wait(met_sem, 4)
+
+    @pl.when(jnp.logical_not(meets_beyond))
+    def _():
+        pl.semaphore_wait(met_sem, 3)
+
+    for step in (2, 1, 3, 0):
+        for i in range(2):
+            first_along_y(step, i, False)
 
     nb_copy = pltpu.make_async_remote_copy(
         nb_own, nb_other, nb_send, nb_sem, device_id=device(partner, f), device_id_type=MESH
@@ -511,6 +544,7 @@
                 pltpu.VMEM((TILES, CHUNK, LANES), BF16),
                 pltpu.SMEM((TILES,), I32),
                 pltpu.SemaphoreType.DMA((7,)),
+                pltpu.SemaphoreType.REGULAR,
                 pltpu.SemaphoreType.DMA,
                 pltpu.SemaphoreType.DMA,
                 pltpu.SemaphoreType.DMA,

time: 35.1 us -> 33.7 us (0.960)
  Pallas kernels: 34.3 us -> 32.9 us
    pallas_call x1, Pallas kernels: 34.3 us -> 32.9 us  [per_device(): pl.pallas_call(functools.partial(kernel, n_tiles), out_shape=pltpu.VMEM(f...]
where the time goes in v6:
time: 33.7 us; the launch traced here: 33.5 us
  Pallas kernels  32.9 us (98%)
  local copies, waits for them, and re-layouts  0.66 us (2%)
    pallas_call x1, Pallas kernels, per_device(): pl.pallas_call(functools.partial(kernel, n_tiles), out_shape=pltpu.VMEM(f...  32.9 us

profile of v6, /device:TPU:1, one launch (start us, length us, event | category | flops | bytes accessed | tf_op | source)
XLA Modules:
  0.0 33.5 jit_solution(3663532216302512681)
XLA Ops:
  0.0 32.9 %shard_map.73 = bf16[32,16,128]{2,1,0:T(8,128)(2,1)S(1)} custom-call(bf16[32,16,128]{2,1,0:T(8,128)(2,1)} %feats_hbm.1, bf16[8,128]{1,0:T(8,128)(2,1)} %weight_hbm.1, f32[1,128]{1,0:T(1,128)} %bitcast.5, s32[16,32]{1,0:T(8,128)} %bitcast.4, s32[32,24,256]{2,1,0:T(8,128)} %bitcast.3, s32[32]{0:T(128)} %counts_hbm.1, s32[1024]{0:T(1024)} %rows_hbm.1), custom_call_target="tpu_custom_call" | custom-call | tf_op jit(solution)/shard_map/pallas_call | solution.py:519
  32.9 0.7 %copy.9 = bf16[32,16,128]{2,1,0:T(8,128)(2,1)} copy(bf16[32,16,128]{2,1,0:T(8,128)(2,1)S(1)} %shard_map.73) | data formatting | bytes 262144

commit v7 on v6

--- a/solution.py
+++ b/solution.py
@@ -105,6 +105,28 @@
     def in_slide(plane):
         return jnp.logical_and(plane >= 0, plane < n_planes)
 
+    def row_exists(w):
+        row = dest_row + w - 2
+        return jnp.logical_and(row >= 0, row < 4 * n_tiles)
+
+    def clear(w, carry):
+        @pl.when(jnp.logical_not(row_exists(w)))
+        def _():
+            win[w] = jnp.zeros((WIN_COLS, 4, 2, 2, CHUNK, LANES), BF16)
+
+        return carry
+
+    lax.fori_loop(0, WIN_ROWS, clear, 0)
+
+    ones_rows = jnp.ones((16, LANES), BF16)
+
+    def fill_ones(i, carry):
+        feats_t[0, i, pl.ds(LANES, 16)] = ones_rows
+        feats_t[1, i, pl.ds(LANES, 16)] = ones_rows
+        return carry
+
+    lax.fori_loop(0, WIN_ROWS * WIN_COLS, fill_ones, 0)
+
     for load in early:
         load.wait()
 
@@ -137,6 +159,7 @@
     def _():
         pl.semaphore_signal(met_sem, inc=1, device_id=device(t - 2, f), device_id_type=MESH)
 
+    parity = (x + y) % 2
     first_y, first_x, second_y, second_x = ([], []), [], [], []
 
     def reaches(r, ahead):
@@ -152,17 +175,17 @@
     def first_along_y(step, i, in_plane):
         to_y = (y + step) % 4
         plane = plane_for(to_y)
-        sent = jnp.logical_and(in_slide(plane), reaches(2 * i, ahead_of(to_y)))
+        sent = jnp.logical_and(in_slide(plane), reaches(2 * i + parity, ahead_of(to_y)))
         sent = jnp.logical_and(sent, (plane == z) == in_plane)
         if in_plane and step == 0:
 
             @pl.when(sent)
             def _():
-                relay_y[i, :, y] = stage_f[2 * i]
+                relay_y[i, :, y] = stage_f[2 * i + parity]
 
             return
         copy = pltpu.make_async_remote_copy(
-            stage_f.at[2 * i], relay_y.at[i, :, y], to_y_send.at[i], to_y_sem.at[i],
+            stage_f.at[2 * i + parity], relay_y.at[i, :, y], to_y_send.at[i], to_y_sem.at[i, y % 2],
             device_id=device(2 * plane + core, 4 * to_y + x), device_id_type=MESH,
         )
         send(copy, sent, first_y[i])
@@ -174,11 +197,11 @@
         for i in range(2):
             columns = pl.ds(2 * (to_x % 2), WIN_COLS)
             if step == 0:
-                relay_x[i, :, x] = stage_f[2 * i + 1, columns]
+                relay_x[i, :, x // 2, x % 2] = stage_f[2 * i + 1 - parity, columns]
             else:
                 copy = pltpu.make_async_remote_copy(
-                    stage_f.at[2 * i + 1, columns], relay_x.at[i, :, x],
-                    to_x_send, to_x_sem.at[i],
+                    stage_f.at[2 * i + 1 - parity, columns], relay_x.at[i, :, x // 2, x % 2],
+                    to_x_send, to_x_sem.at[i, x % 2],
                     device_id=device(t, 4 * y + to_x), device_id_type=MESH,
                 )
                 send(copy, True, first_x)
@@ -249,99 +272,79 @@
 
     lax.fori_loop(1, 16, start_weight, 0)
 
-    def row_exists(w):
-        row = dest_row + w - 2
-        return jnp.logical_and(row >= 0, row < 4 * n_tiles)
-
-    def clear(w, carry):
-        @pl.when(jnp.logical_not(row_exists(w)))
-        def _():
-            win[w] = jnp.zeros((WIN_COLS, 4, 4, CHUNK, LANES), BF16)
-
-        return carry
-
-    lax.fori_loop(0, WIN_ROWS, clear, 0)
-
-    ones_rows = jnp.ones((16, LANES), BF16)
-
-    def fill_ones(i, carry):
-        feats_t[0, i, pl.ds(LANES, 16)] = ones_rows
-        feats_t[1, i, pl.ds(LANES, 16)] = ones_rows
-        return carry
-
-    lax.fori_loop(0, WIN_ROWS * WIN_COLS, fill_ones, 0)
-
     my_cells = pl.ds(pl.multiple_of(f * CHUNK, CHUNK), CHUNK)
     ahead = ahead_of(y)
     band_plane = z + jnp.logical_and(core == 0, y == 3).astype(I32) - jnp.logical_and(
         core == 1, y == 0).astype(I32)
 
     for i in range(2):
-        r = 2 * i
-        here = jnp.logical_and(in_slide(band_plane), reaches(r, ahead))
-
-        @pl.when(jnp.logical_and(here, band_plane != z))
-        def _():
-            settle(to_y_sem.at[i], relay_y.at[i])
-
-        @pl.when(jnp.logical_and(here, band_plane == z))
-        def _():
-            settle(to_y_sem.at[i], relay_y.at[i, :, pl.ds(0, 3)])
-
-        for step in (2, 1, 3, 0):
-            to_x = (x + step) % 4
-            gap = ahead + to_x // 2 - r
-            w = jnp.clip(2 - gap, 0, WIN_ROWS - 1)
-            columns = pl.ds(2 * (to_x % 2), WIN_COLS)
-            needed = jnp.logical_and(here, jnp.logical_and(gap >= -2, gap <= 2))
-            for q in range(2):
-                sent = needed
+        for odd in range(2):
+            r = 2 * i + (x + odd) % 2
+            here = jnp.logical_and(in_slide(band_plane), reaches(r, ahead))
+            own = jnp.logical_and(band_plane == z, y % 2 == odd)
+
+            @pl.when(jnp.logical_and(here, jnp.logical_not(own)))
+            def _():
+                settle(to_y_sem.at[i, odd], relay_y.at[i, :, pl.ds(0, 2)])
+
+            @pl.when(jnp.logical_and(here, own))
+            def _():
+                settle(to_y_sem.at[i, odd], relay_y.at[i, :, pl.ds(0, 1)])
+
+            for step in (2, 1, 3, 0):
+                to_x = (x + step) % 4
+                gap = ahead + to_x // 2 - r
+                w = jnp.clip(2 - gap, 0, WIN_ROWS - 1)
+                columns = pl.ds(2 * (to_x % 2), WIN_COLS)
+                needed = jnp.logical_and(here, jnp.logical_and(gap >= -2, gap <= 2))
+                for q in range(2):
+                    source_y = 2 * q + odd
+                    sent = needed
+                    if step == 0:
+                        sent = jnp.logical_and(needed, core != q)
+
+                        @pl.when(jnp.logical_and(needed, core == q))
+                        def _():
+                            win[w, :, source_y, x // 2, x % 2] = relay_y[i, columns, source_y]
+
+                    copy = pltpu.make_async_remote_copy(
+                        relay_y.at[i, columns, source_y], win.at[w, :, source_y, x // 2, x % 2],
+                        win_y_send, win_sem.at[w],
+                        device_id=device(2 * z + q, 4 * y + to_x), device_id_type=MESH,
+                    )
+                    send(copy, sent, second_y)
+
+        for odd in range(2):
+            r = 2 * i + 1 - (y + odd) % 2
+
+            @pl.when(x % 2 == odd)
+            def _():
+                settle(to_x_sem.at[i, odd], relay_x.at[i, :, pl.ds(0, 1), odd])
+
+            @pl.when(x % 2 != odd)
+            def _():
+                settle(to_x_sem.at[i, odd], relay_x.at[i, :, :, odd])
+
+            for step in (2, 1, 3, 0):
+                to_y = (y + step) % 4
+                plane = plane_for(to_y)
+                gap = ahead_of(to_y) + x // 2 - r
+                w = jnp.clip(2 - gap, 0, WIN_ROWS - 1)
+                sent = jnp.logical_and(in_slide(plane), jnp.logical_and(gap >= -2, gap <= 2))
                 if step == 0:
-                    sent = jnp.logical_and(needed, core != q)
-
-                    @pl.when(jnp.logical_and(needed, core == q))
+                    at_home = jnp.logical_and(plane == z, home == core)
+                    mine = jnp.logical_and(sent, at_home)
+                    sent = jnp.logical_and(sent, jnp.logical_not(at_home))
+
+                    @pl.when(mine)
                     def _():
-                        win[w, :, 2 * q : 2 * q + 2, x] = relay_y[i, columns, 2 * q : 2 * q + 2]
+                        win[w, :, y, :, odd] = relay_x[i, :, :, odd]
 
                 copy = pltpu.make_async_remote_copy(
-                    relay_y.at[i, columns, pl.ds(2 * q, 2)], win.at[w, :, pl.ds(2 * q, 2), x],
-                    win_y_send, win_sem.at[w],
-                    device_id=device(2 * z + q, 4 * y + to_x), device_id_type=MESH,
+                    relay_x.at[i, :, :, odd], win.at[w, :, y, :, odd], win_x_send, win_sem.at[w],
+                    device_id=device(2 * plane + home, 4 * to_y + x), device_id_type=MESH,
                 )
-                send(copy, sent, second_y)
-
-        r = 2 * i + 1
-        settle(to_x_sem.at[i], relay_x.at[i, :, pl.ds(0, 3)])
-
-        for step in (2, 1, 3, 0):
-            to_y = (y + step) % 4
-            plane = plane_for(to_y)
-            gap = ahead_of(to_y) + x // 2 - r
-            w = jnp.clip(2 - gap, 0, WIN_ROWS - 1)
-            sent = jnp.logical_and(in_slide(plane), jnp.logical_and(gap >= -2, gap <= 2))
-            if step == 0:
-                at_home = jnp.logical_and(plane == z, home == core)
-                mine = jnp.logical_and(sent, at_home)
-                sent = jnp.logical_and(sent, jnp.logical_not(at_home))
-
-                @pl.when(mine)
-                def _():
-                    win[w, :, y] = relay_x[i]
-
-            copy = pltpu.make_async_remote_copy(
-                relay_x.at[i], win.at[w, :, y], win_x_send, win_sem.at[w],
-                device_id=device(2 * plane + home, 4 * to_y + x), device_id_type=MESH,
-            )
-            send(copy, sent, second_x)
-
-    def invert(r, carry):
-        found = 0
-        for s in range(1, TILES):
-            found = found + jnp.where(rows_ref[t * TILES + s] == t * TILES + r, s, 0)
-        inverse[r] = jnp.clip(found, 0, TILES - 1)
-        return carry
-
-    lax.fori_loop(0, TILES, invert, 0)
+                send(copy, sent, second_x)
 
     def unpack(k, carry):
         with_mine = jnp.logical_and(k == f // 4 * 4, core == home)
@@ -379,21 +382,19 @@
     def forward(w, carry):
         from_here = (dest_row + w - 2) // 4 == t
         from_chip = (dest_row + w - 2) // 4 % 2 == core
-        even = (dest_row + w) % 2 == 0
-
-        part_here = jnp.where(even, from_chip, jnp.logical_and(from_here, home == core))
-
-        @pl.when(jnp.logical_and(row_exists(w), jnp.logical_not(part_here)))
-        def _():
-            settle(win_sem.at[w], win.at[w, :, kept])
-
-        @pl.when(jnp.logical_and(row_exists(w), jnp.logical_and(part_here, even)))
-        def _():
-            settle(win_sem.at[w], win.at[w, :, kept, pl.ds(0, 3)])
-
-        @pl.when(jnp.logical_and(row_exists(w), jnp.logical_and(part_here, jnp.logical_not(even))))
-        def _():
-            settle(win_sem.at[w], win.at[w, :, 2 * core])
+        from_here = jnp.logical_and(from_here, home == core)
+
+        @pl.when(jnp.logical_and(row_exists(w), jnp.logical_not(from_chip)))
+        def _():
+            settle(win_sem.at[w], words_v.at[pl.ds(0, 8)])
+
+        @pl.when(jnp.logical_and(row_exists(w), jnp.logical_and(from_chip, jnp.logical_not(from_here))))
+        def _():
+            settle(win_sem.at[w], words_v.at[pl.ds(0, 7)])
+
+        @pl.when(jnp.logical_and(row_exists(w), from_here))
+        def _():
+            settle(win_sem.at[w], words_v.at[pl.ds(0, 5)])
 
         @pl.when(row_exists(w))
         def _():
@@ -473,13 +474,22 @@
     def _():
         obuf[pl.ds(first_out, 2)] = stage_o[:, my_cells]
 
+    def invert(r, carry):
+        found = 0
+        for s in range(1, TILES):
+            found = found + jnp.where(rows_ref[t * TILES + s] == t * TILES + r, s, 0)
+        inverse[r] = jnp.clip(found, 0, TILES - 1)
+        return carry
+
+    lax.fori_loop(0, TILES, invert, 0)
+
     nb_copy.wait_send()
     settle(weight_send, wall.at[pl.ds(0, 15)])
     for i in range(2):
         settle_count(to_y_send.at[i], first_y[i], 3, lambda n: relay_y.at[0, :, pl.ds(0, n)])
-    settle(to_x_send, relay_x.at[:, :, pl.ds(0, 3)])
-    settle_count(win_y_send, second_y, 16, lambda n: words_v.at[pl.ds(0, 2 * n)])
-    settle_count(win_x_send, second_x, 8, lambda n: words_v.at[pl.ds(0, 4 * n)])
+    settle(to_x_send, words_v.at[pl.ds(0, 6)])
+    settle_count(win_y_send, second_y, 28, lambda n: words_v.at[pl.ds(0, n)])
+    settle_count(win_x_send, second_x, 10, lambda n: words_v.at[pl.ds(0, 2 * n)])
     settle_count(
         fwd_send, [row_exists(w) for w in range(WIN_ROWS)], WIN_ROWS, lambda n: win.at[pl.ds(0, n), :, kept]
     )
@@ -533,8 +543,8 @@
                 pltpu.VMEM((4, 8, CHUNK, LANES), BF16),
                 pltpu.VMEM((TILES, WORDS, LANES), I32),
                 pltpu.VMEM((2, 8, 4, CHUNK, LANES), BF16),
-                pltpu.VMEM((2, WIN_COLS, 4, CHUNK, LANES), BF16),
-                pltpu.VMEM((WIN_ROWS, WIN_COLS, 4, 4, CHUNK, LANES), BF16),
+                pltpu.VMEM((2, WIN_COLS, 2, 2, CHUNK, LANES), BF16),
+                pltpu.VMEM((WIN_ROWS, WIN_COLS, 4, 2, 2, CHUNK, LANES), BF16),
                 pltpu.VMEM((SLOTS, 2, WORDS, LANES), I32),
                 pltpu.VMEM((16, 8, LANES), BF16),
                 pltpu.VMEM((2, WORDS * BITS, LANES), I32),
@@ -552,9 +562,9 @@
                 pltpu.SemaphoreType.DMA,
                 pltpu.SemaphoreType.DMA,
                 pltpu.SemaphoreType.DMA((2,)),
-                pltpu.SemaphoreType.DMA((2,)),
-                pltpu.SemaphoreType.DMA,
-                pltpu.SemaphoreType.DMA((2,)),
+                pltpu.SemaphoreType.DMA((2, 2)),
+                pltpu.SemaphoreType.DMA,
+                pltpu.SemaphoreType.DMA((2, 2)),
                 pltpu.SemaphoreType.DMA,
                 pltpu.SemaphoreType.DMA,
                 pltpu.SemaphoreType.DMA((WIN_ROWS,)),

time: 33.7 us -> 32.4 us (0.961)
  Pallas kernels: 32.9 us -> 31.6 us
    pallas_call x1, Pallas kernels: 32.9 us -> 31.6 us  [per_device(): pl.pallas_call(functools.partial(kernel, n_tiles), out_shape=pltpu.VMEM(f...]
where the time goes in v7:
time: 32.4 us; the launch traced here: 32.3 us
  Pallas kernels  31.6 us (98%)
  local copies, waits for them, and re-layouts  0.66 us (2%)
    pallas_call x1, Pallas kernels, per_device(): pl.pallas_call(functools.partial(kernel, n_tiles), out_shape=pltpu.VMEM(f...  31.6 us
    unnamed x1, local copies, waits for them, and re-layouts  0.66 us

profile of v7, /device:TPU:1, one launch (start us, length us, event | category | flops | bytes accessed | tf_op | source)
XLA Modules:
  0.0 32.3 jit_solution(2876723760094407413)
XLA Ops:
  0.0 31.6 %shard_map.73 = bf16[32,16,128]{2,1,0:T(8,128)(2,1)S(1)} custom-call(bf16[32,16,128]{2,1,0:T(8,128)(2,1)} %feats_hbm.1, bf16[8,128]{1,0:T(8,128)(2,1)} %weight_hbm.1, f32[1,128]{1,0:T(1,128)} %bitcast.5, s32[16,32]{1,0:T(8,128)} %bitcast.4, s32[32,24,256]{2,1,0:T(8,128)} %bitcast.3, s32[32]{0:T(128)} %counts_hbm.1, s32[1024]{0:T(1024)} %rows_hbm.1), custom_call_target="tpu_custom_call" | custom-call | tf_op jit(solution)/shard_map/pallas_call | solution.py:529
  31.6 0.7 %copy.9 = bf16[32,16,128]{2,1,0:T(8,128)(2,1)} copy(bf16[32,16,128]{2,1,0:T(8,128)(2,1)S(1)} %shard_map.73) | data formatting | bytes 262144
